TPU v7x, 32 devices: a whole 2x2x4 slice. The times are simulated.
32 devices in a mesh: gz: 2 (over z_hi), gy: 4 (over z_lo, core), gx: 4 (over y, x).
Axes of the slice: x: 2, y: 2, z: 4 (z_hi: 2, z_lo: 2; z = z_hi * 2 + z_lo), core: 2. Of those that a mesh axis runs over, the one named last changes fastest.
Arguments:
- charges: float32 [65536], P(('gz', 'gy', 'gx')), may hold values from -2.5 to 2.5
- fractions: float32 [3, 65536], P(None, ('gz', 'gy', 'gx')), may hold values from 0 to 1
- base_cells: int32 [3, 65536], P(None, ('gz', 'gy', 'gx')), may hold values from 0 to 255, as said below
- counts: int32 [2, 4, 4], P('gz', 'gy', 'gx'), may hold values from 1024 to 2048, as said below
Outputs:
- forces: float32 [3, 65536], P(None, ('gz', 'gy', 'gx'))
Inputs may be any that keep to these rules, and one draw needn't show every extreme that they name: `base_cells`: atom slots of the block at gz, gy, gx have base cells inside that block's cells: x in gx*64 to gx*64 + 63, y in gy*64 to gy*64 + 63, z in gz*128 to gz*128 + 127. The first counts[b] slots of block b hold atoms, the rest are empty; some block is full in every draw.
All inputs are finite; a program needn't handle non-finite values.
Results may differ from a plain program's by a relative error of at most 0.0003.
Values sent between devices are 32-bit elements; how exact they have to be, the bound alone decides.
A program may use at most 256 MiB of HBM per device.

v0:
```python
import functools

import jax
import jax.numpy as jnp
import numpy as np
from jax import lax
from jax.experimental import pallas as pl
from jax.experimental.pallas import tpu as pltpu
from jax.sharding import PartitionSpec as P

GRID = 256
ORDER = 4


coulomb = 332.0636
ewald = 0.7
highest = lax.Precision.HIGH
gather_rows = 4


def from_behind(value, axis, steps):
    count = lax.axis_size(axis)
    pairs = [(source, (source + steps) % count) for source in range(count)]
    return lax.ppermute(value, axis, pairs)


def spline_weights(frac):
    rest = 1.0 - frac
    square = frac * frac
    cube = square * frac
    weights = jnp.stack(
        [
            rest * rest * rest / 6.0,
            (3.0 * cube - 6.0 * square + 4.0) / 6.0,
            (-3.0 * cube + 3.0 * square + 3.0 * frac + 1.0) / 6.0,
            cube / 6.0,
        ]
    )
    slopes = jnp.stack(
        [-0.5 * rest * rest, 1.5 * square - 2.0 * frac, -1.5 * square + frac + 0.5, 0.5 * square]
    )
    return (weights, slopes)


def green_factors(index, length):
    signed = jnp.where(2 * index < length, index, index - length).astype(jnp.float32)
    bspline = 36.0 / (4.0 + 2.0 * jnp.cos(index.astype(jnp.float32) * (2.0 * jnp.pi / length))) ** 2
    bspline = jnp.where(2 * index == length, 0.0, bspline)
    return (signed * signed, bspline)


def place_rows(values, lowest, length):
    offset = jnp.arange(length, dtype=jnp.int32)[:, None] - lowest[None, :]
    placed = jnp.zeros((length, lowest.shape[0]), jnp.float32)
    for order_index in range(values.shape[0]):
        placed = placed + jnp.where(offset == order_index, values[order_index][None, :], 0.0)
    return placed


def halves(value):
    high = value.astype(jnp.bfloat16)
    low = (value - high.astype(jnp.float32)).astype(jnp.bfloat16)
    return (high, low)


def rounded_halves(value):
    high = lax.reduce_precision(value, exponent_bits=8, mantissa_bits=7)
    return (high.astype(jnp.bfloat16), (value - high).astype(jnp.bfloat16))


def round_up(value, unit):
    return -(-value // unit) * unit


def spread_kernel(x_ref, y_ref, high_ref, low_ref, out_ref):
    contract = (((1,), (1,)), ((), ()))
    block, pad_y, span_z = out_ref.shape
    lines = y_ref[...]
    pairs = jnp.concatenate([x_ref[i] * lines for i in range(block)], axis=0)
    high, low = halves(pairs)
    rows = high.shape[0]
    both = jnp.concatenate([high, low], axis=0)
    product = lax.dot_general(both, high_ref[...], contract, preferred_element_type=jnp.float32)
    rest = lax.dot_general(high, low_ref[...], contract, preferred_element_type=jnp.float32)
    total = product[:rows] + (product[rows:] + rest)
    out_ref[...] = total.reshape(block, pad_y, span_z)


def spread(rows_x, rows_y, weighted_z):
    span_x, capacity = rows_x.shape
    pad_y = rows_y.shape[0]
    span_z = weighted_z.shape[0]
    high, low = rounded_halves(weighted_z)
    return pl.pallas_call(
        spread_kernel,
        grid=(span_x // gather_rows,),
        in_specs=[
            pl.BlockSpec((gather_rows, 1, capacity), lambda i: (i, 0, 0)),
            pl.BlockSpec((pad_y, capacity), lambda i: (0, 0)),
            pl.BlockSpec((span_z, capacity), lambda i: (0, 0)),
            pl.BlockSpec((span_z, capacity), lambda i: (0, 0)),
        ],
        out_specs=pl.BlockSpec((gather_rows, pad_y, span_z), lambda i: (i, 0, 0)),
        out_shape=jax.ShapeDtypeStruct((span_x, pad_y, span_z), jnp.float32),
    )(rows_x[:, None, :], rows_y, high, low)


def gather_kernel(width, pot_ref, z_ref, gz_ref, y_ref, gy_ref, x_ref, gx_ref, out_ref):
    block, pad_y, depth = pot_ref.shape
    capacity = out_ref.shape[1]

    @pl.when(pl.program_id(0) == 0)
    def _():
        out_ref[...] = jnp.zeros_like(out_ref)

    pot = pot_ref[...].reshape(block * pad_y, depth)

    def chunk(c, carry):
        here = pl.ds(pl.multiple_of(c * width, width), width)
        plain = jnp.dot(pot, z_ref[:, here], preferred_element_type=jnp.float32)
        sloped = jnp.dot(pot, gz_ref[:, here], preferred_element_type=jnp.float32)
        weight = y_ref[:, here]
        slope = gy_ref[:, here]
        force_x = out_ref[0:1, here]
        force_y = out_ref[1:2, here]
        force_z = out_ref[2:3, here]
        for i in range(block):
            rows = slice(i * pad_y, (i + 1) * pad_y)
            part = plain[rows]
            row_x = x_ref[i, :, here]
            force_x += gx_ref[i, :, here] * jnp.sum(weight * part, axis=0, keepdims=True)
            force_y += row_x * jnp.sum(slope * part, axis=0, keepdims=True)
            force_z += row_x * jnp.sum(weight * sloped[rows], axis=0, keepdims=True)
        out_ref[0:1, here] = force_x
        out_ref[1:2, here] = force_y
        out_ref[2:3, here] = force_z
        return carry

    lax.fori_loop(0, capacity // width, chunk, 0)


def gather(potential, rows_x, grads_x, rows_y, grads_y, rows_z, grads_z):
    span_x, span_y, span_z = potential.shape
    capacity = rows_x.shape[1]
    pad_y = rows_y.shape[0]
    pad_x = rows_x.shape[0]
    high, low = rounded_halves(potential)
    stacked = jnp.concatenate([high, low, high], axis=2)
    stacked = jnp.pad(stacked, ((0, pad_x - span_x), (0, pad_y - span_y), (0, 0)))
    high, low = rounded_halves(rows_z)
    table = jnp.concatenate([high, high, low], axis=0)
    high, low = rounded_halves(grads_z)
    slope_table = jnp.concatenate([high, high, low], axis=0)
    depth = 3 * span_z

    def whole(rows):
        return pl.BlockSpec((rows, capacity), lambda i: (0, 0))

    line = pl.BlockSpec((gather_rows, 1, capacity), lambda i: (i, 0, 0))
    return pl.pallas_call(
        functools.partial(gather_kernel, 256),
        grid=(pad_x // gather_rows,),
        in_specs=[
            pl.BlockSpec((gather_rows, pad_y, depth), lambda i: (i, 0, 0)),
            whole(depth),
            whole(depth),
            whole(pad_y),
            whole(pad_y),
            line,
            line,
        ],
        out_specs=pl.BlockSpec((3, capacity), lambda i: (0, 0)),
        out_shape=jax.ShapeDtypeStruct((3, capacity), jnp.float32),
    )(stacked, table, slope_table, rows_y, grads_y, rows_x[:, None, :], grads_x[:, None, :])


def y_shift(data, by):
    return from_behind(data, "gy", by)


def z_shift(data, by):
    return from_behind(data, "gz", by)


def exchange(data, axes):
    return lax.all_to_all(data, axes, split_axis=0, concat_axis=0, tiled=True)


def complex_turn(outputs, inputs, sign):
    angle = outputs[:, None] * inputs[None, :] % GRID * (2.0 * np.pi / GRID)
    cosine, sine = np.cos(angle), sign * np.sin(angle)
    return np.array([[cosine, -sine], [sine, cosine]])


def turn(table, data):
    return jnp.dot(
        jnp.asarray(table, jnp.float32),
        data,
        precision=highest,
        preferred_element_type=jnp.float32,
    )


def per_device(charges, fractions, base_cells, counts):

    def x_shift(data, by):
        return from_behind(data, "gx", by)

    count_x = lax.axis_size("gx")
    count_y = lax.axis_size("gy")
    count_z = lax.axis_size("gz")
    index_x = lax.axis_index("gx")
    index_y = lax.axis_index("gy")
    index_z = lax.axis_index("gz")
    cells_x = GRID // count_x
    cells_y = GRID // count_y
    cells_z = GRID // count_z
    ghost_width = ORDER - 1
    span_x = cells_x + ghost_width
    span_y = cells_y + ghost_width
    span_z = cells_z + ghost_width
    planes = count_x * count_y
    width_b = cells_x // count_y
    kept = GRID // 2
    width_k = kept // planes
    width_u = GRID // count_z
    capacity = charges.shape[0]
    live = jnp.arange(capacity, dtype=jnp.int32) < counts.reshape(())
    charge = jnp.where(live, charges, jnp.zeros_like(charges))
    weights_x, slopes_x = spline_weights(fractions[0])
    weights_y, slopes_y = spline_weights(fractions[1])
    weights_z, slopes_z = spline_weights(fractions[2])
    lowest_x = base_cells[0] - index_x * cells_x
    lowest_y = base_cells[1] - index_y * cells_y
    lowest_z = base_cells[2] - index_z * cells_z
    pad_x = round_up(span_x, gather_rows)
    pad_y = round_up(span_y, 16)
    rows_x = place_rows(weights_x, lowest_x, pad_x)
    grads_x = place_rows(slopes_x, lowest_x, pad_x)
    rows_y = place_rows(weights_y, lowest_y, pad_y)
    grads_y = place_rows(slopes_y, lowest_y, pad_y)
    rows_z = place_rows(weights_z, lowest_z, span_z)
    grads_z = place_rows(slopes_z, lowest_z, span_z)
    grid = spread(rows_x, rows_y, rows_z * charge[None, :])[:span_x, :span_y]
    arrived = z_shift(grid[:, :, cells_z:], 1)
    grid = jnp.concatenate(
        [grid[:, :, :ghost_width] + arrived, grid[:, :, ghost_width:cells_z]], axis=2
    )
    arrived = x_shift(grid[cells_x:], 1)
    grid = jnp.concatenate([grid[:ghost_width] + arrived, grid[ghost_width:cells_x]], axis=0)
    arrived = y_shift(grid[:, cells_y:], 1)
    grid = jnp.concatenate([grid[:, :ghost_width] + arrived, grid[:, ghost_width:cells_y]], axis=1)
    cell_index = jnp.arange(GRID, dtype=jnp.int32)
    cells = np.arange(GRID)

    data = exchange(grid.reshape(count_y, width_b, cells_y, cells_z), "gy")
    data = data.transpose(0, 2, 1, 3).reshape(GRID, width_b * cells_z)
    table = complex_turn(np.arange(kept), cells, -1.0)[:, 0]
    table = table.reshape(2, planes, width_k, GRID).transpose(1, 0, 2, 3)
    data = turn(table.reshape(2 * kept, GRID), data)
    data = exchange(data.reshape(planes, 2 * width_k, width_b * cells_z), ("gx", "gy"))
    data = data.reshape(planes, 2, width_k, width_b, cells_z).transpose(0, 1, 3, 2, 4)
    table = complex_turn(cells, cells, -1.0).reshape(2, 2, count_z, width_u, planes, width_b)
    table = table.transpose(2, 0, 3, 4, 1, 5).reshape(2 * GRID, 2 * GRID)
    data = turn(table, data.reshape(2 * GRID, width_k * cells_z))
    data = exchange(data.reshape(count_z, 2 * width_u, width_k * cells_z), "gz")
    data = data.reshape(count_z, 2, width_u, width_k, cells_z).transpose(0, 1, 4, 3, 2)
    table = complex_turn(cells, cells, -1.0).reshape(2, 2, GRID, count_z, cells_z)
    table = table.transpose(0, 2, 3, 1, 4).reshape(2 * GRID, 2 * GRID)
    data = turn(table, data.reshape(2 * GRID, width_k * width_u))
    data = data.reshape(2, GRID, width_k * width_u)
    index_ky = (index_x * count_y + index_y) * width_k + jnp.arange(width_k, dtype=jnp.int32)
    index_kx = index_z * width_u + jnp.arange(width_u, dtype=jnp.int32)
    square_y, spline_y = green_factors(index_ky, GRID)
    square_x, spline_x = green_factors(index_kx, GRID)
    square_z, spline_z = green_factors(cell_index, GRID)
    square_yx = (square_y[:, None] + square_x[None, :]).reshape(-1)
    factor_yx = (spline_y[:, None] * spline_x[None, :]).reshape(-1)
    square = square_z[:, None] + square_yx[None, :]
    factor = spline_z[:, None] * factor_yx[None, :]
    green = jnp.where(
        square > 0.0,
        coulomb
        * jnp.exp(square * (-jnp.pi**2 / (ewald * ewald * GRID * GRID)))
        * factor
        / (jnp.pi * GRID * jnp.maximum(square, 1.0)),
        0.0,
    )
    data = data * green[None]
    table = complex_turn(cells, cells, 1.0).reshape(2, 2, count_z, cells_z, GRID)
    table = table.transpose(2, 0, 3, 1, 4).reshape(2 * GRID, 2 * GRID)
    data = turn(table, data.reshape(2 * GRID, width_k * width_u))
    data = exchange(data.reshape(count_z, 2 * cells_z, width_k * width_u), "gz")
    data = data.reshape(count_z, 2, cells_z, width_k, width_u).transpose(0, 1, 4, 3, 2)
    table = complex_turn(cells, cells, 1.0).reshape(2, 2, planes, width_b, count_z, width_u)
    table = table.transpose(2, 0, 3, 4, 1, 5).reshape(2 * GRID, 2 * GRID)
    data = turn(table, data.reshape(2 * GRID, width_k * cells_z))
    data = exchange(data.reshape(planes, 2 * width_b, width_k * cells_z), ("gx", "gy"))
    data = data.reshape(planes, 2, width_b, width_k, cells_z).transpose(0, 1, 3, 2, 4)
    table = complex_turn(cells, np.arange(kept), 1.0)[0]
    table = table * np.where(np.arange(kept) > 0, 2.0, 1.0)
    table = table.reshape(2, GRID, planes, width_k).transpose(1, 2, 0, 3)
    data = turn(table.reshape(GRID, 2 * kept), data.reshape(2 * kept, width_b * cells_z))
    data = exchange(data.reshape(count_y, cells_y, width_b * cells_z), "gy")
    potential = data.reshape(count_y, cells_y, width_b, cells_z).transpose(0, 2, 1, 3)
    potential = potential.reshape(cells_x, cells_y, cells_z)
    arrived = x_shift(potential[:ghost_width], -1)
    potential = jnp.concatenate([potential, arrived], axis=0)
    arrived = y_shift(potential[:, :ghost_width], -1)
    potential = jnp.concatenate([potential, arrived], axis=1)
    arrived = z_shift(potential[:, :, :ghost_width], -1)
    potential = jnp.concatenate([potential, arrived], axis=2)
    return -charge[None, :] * gather(
        potential, rows_x, grads_x, rows_y, grads_y, rows_z, grads_z
    )


def solution(mesh):
    in_specs = (
        P(("gz", "gy", "gx")),
        P(None, ("gz", "gy", "gx")),
        P(None, ("gz", "gy", "gx")),
        P("gz", "gy", "gx"),
    )
    out_specs = P(None, ("gz", "gy", "gx"))
    return jax.shard_map(
        per_device, mesh=mesh, in_specs=in_specs, out_specs=out_specs, check_vma=False
    )
```

profile of v0, /device:TPU:0, one launch (start us, length us, event | category | flops | bytes accessed | tf_op | source)
XLA Modules:
  0.0 396.8 jit_solution(926266849055088889)
XLA Ops:
  4.2 3.7 fusion.47
  9.3 2.9 reduce-precision_convert_fusion.1
  12.2 22.9 %shard_map.100 = f32[68,80,131]{2,1,0:T(8,128)} custom-call(f32[68,1,2048]{2,1,0:T(1,128)} %get-tuple-element.45.x_ref, f32[80,2048]{1,0:T(8,128)} %get-tuple-element.47.y_ref, bf16[131,2048]{1,0:T(8,128)(2,1)} %get-tuple-element.49.high_ref, bf16[131,2048]{1,0:T(8,128)(2,1)} %get-tuple-element.48.low_ref), custom_call_target="tpu_custom_call" | custom-call | tf_op jit(solution)/shard_map/pallas_call | solution.py:94
  37.9 4.1 %collective-permute-start = (f32[67,67,3]{1,0,2:T(8,128)S(1)}, f32[67,67,3]{1,0,2:T(8,128)S(1)}, u32[]{:S(2)}, u32[]{:S(2)}) collective-permute-start(f32[67,67,3]{1,0,2:T(8,128)S(1)} %copy.17), channel_id=1, source_target_pairs={{0,16},{16,0},{1,17},{17,1},{2,18},{18,2},{3,19},{19,3},{4,20},{20... | collective-permute-start | bytes 161612 | tf_op jit(solution)/shard_map/ppermute | solution.py:24
  44.4 3.0 collective-permute-done
  49.8 2.7 slice_add_fusion
  54.2 4.1 %collective-permute-done.1 = f32[3,67,128]{2,1,0:T(8,128)S(1)} collective-permute-done((f32[3,67,128]{2,1,0:T(8,128)S(1)}, f32[3,67,128]{2,1,0:T(8,128)S(1)}, u32[]{:S(2)}, u32[]{:S(2)}) %collective-permute-start.1) | collective-permute-done | bytes 102944 | tf_op jit(solution)/shard_map/ppermute | solution.py:24
  59.5 4.1 %collective-permute-done.2 = f32[64,3,128]{2,1,0:T(4,128)S(1)} collective-permute-done((f32[64,3,128]{2,1,0:T(4,128)S(1)}, f32[64,3,128]{2,1,0:T(4,128)S(1)}, u32[]{:S(2)}, u32[]{:S(2)}) %collective-permute-start.2) | collective-permute-done | bytes 98336 | tf_op jit(solution)/shard_map/ppermute | solution.py:24
  65.3 28.3 %all_to_all.30 = f32[4,16,64,128]{3,1,2,0:T(8,128)S(1)} all-to-all(f32[4,16,64,128]{3,1,2,0:T(8,128)S(1)} %copy.19), channel_id=1, replica_groups=mesh['gz'=2,'gy'=4,'gx'=4] {'gy'}, dimensions={0} | all-to-all | bytes 4194304 | tf_op jit(solution)/shard_map/all_to_all | solution.py:186
  95.2 30.3 %all_to_all.31 = f32[16,16,2048]{2,1,0:T(8,128)S(1)} all-to-all(f32[16,16,2048]{2,1,0:T(8,128)S(1)} %bitcast.113), channel_id=1, replica_groups=mesh['gz'=2,'gy'=4,'gx'=4] {'gx','gy'}, dimensions={0} | all-to-all | bytes 4194304 | tf_op jit(solution)/shard_map/all_to_all | solution.py:186
  125.5 3.3 fusion.17
  128.8 4.1 %all-to-all-start.2 = ((f32[2,256,1024]{2,1,0:T(8,128)}), f32[2,256,1024]{2,1,0:T(8,128)S(1)}, u32[]{:S(2)}, u32[]{:S(2)}) async-start(f32[2,256,1024]{2,1,0:T(8,128)} %bitcast.110), calls=%async_computation.2 | async-start | bytes 4194304 | tf_op jit(solution)/shard_map/all_to_all | solution.py:186
  133.8 46.6 %all-to-all-done.2 = f32[2,256,1024]{2,1,0:T(8,128)S(1)} async-done(((f32[2,256,1024]{2,1,0:T(8,128)}), f32[2,256,1024]{2,1,0:T(8,128)S(1)}, u32[]{:S(2)}, u32[]{:S(2)}) %all-to-all-start.2) | async-done | bytes 2097184 | tf_op jit(solution)/shard_map/all_to_all | solution.py:186
  184.3 3.4 bitcast_multiply_fusion
  189.6 48.8 %all_to_all.32 = f32[2,256,1024]{2,1,0:T(8,128)S(1)} all-to-all(f32[2,256,1024]{2,1,0:T(8,128)S(1)} %bitcast.115), channel_id=1, replica_groups=mesh['gz'=2,'gy'=4,'gx'=4] {'gz'}, dimensions={0} | all-to-all | bytes 4194304 | tf_op jit(solution)/shard_map/all_to_all | solution.py:186
  244.4 30.6 %all_to_all.33 = f32[16,32,1024]{2,1,0:T(8,128)S(1)} all-to-all(f32[16,32,1024]{2,1,0:T(8,128)S(1)} %bitcast.117), channel_id=1, replica_groups=mesh['gz'=2,'gy'=4,'gx'=4] {'gx','gy'}, dimensions={0} | all-to-all | bytes 4194304 | tf_op jit(solution)/shard_map/all_to_all | solution.py:186
  277.2 28.1 %all_to_all.34 = f32[4,64,2048]{2,1,0:T(8,128)S(1)} all-to-all(f32[4,64,2048]{2,1,0:T(8,128)S(1)} %bitcast.119), channel_id=1, replica_groups=mesh['gz'=2,'gy'=4,'gx'=4] {'gy'}, dimensions={0} | all-to-all | bytes 4194304 | tf_op jit(solution)/shard_map/all_to_all | solution.py:186
  307.1 4.1 %collective-permute-done.3 = f32[3,64,128]{2,1,0:T(8,128)S(1)} collective-permute-done((f32[3,64,128]{2,1,0:T(8,128)S(1)}, f32[3,64,128]{2,1,0:T(8,128)S(1)}, u32[]{:S(2)}, u32[]{:S(2)}) %collective-permute-start.3) | collective-permute-done | bytes 98336 | tf_op jit(solution)/shard_map/ppermute | solution.py:24
  315.5 3.3 copy.23
  319.2 3.4 pad_maximum_fusion.4
  322.6 5.5 %collective-permute-done.5 = f32[67,67,3]{1,0,2:T(8,128)} collective-permute-done((f32[67,67,3]{1,0,2:T(8,128)}, f32[67,67,3]{1,0,2:T(8,128)}, u32[]{:S(2)}, u32[]{:S(2)}) %collective-permute-start.5) | collective-permute-done | bytes 53900 | tf_op jit(solution)/shard_map/ppermute | solution.py:24
  328.0 3.2 copy.24
  333.8 8.2 %fusion.8.pot_ref = bf16[68,80,393]{2,1,0:T(8,128)(2,1)} fusion(bf16[67,67,131]{2,1,0:T(8,128)(2,1)S(1)} %get-tuple-element.8, bf16[67,67,131]{2,1,0:T(8,128)(2,1)S(1)} %get-tuple-element.7), kind=kLoop, calls=%fused_computation.12 | loop fusion | flops 32068800 | bytes 6628076 | tf_op jit(solution)/shard_map/concatenate | solution.py:148
  342.0 53.4 %shard_map.101 = f32[3,2048]{1,0:T(4,128)} custom-call(bf16[68,80,393]{2,1,0:T(8,128)(2,1)} %fusion.8.pot_ref, bf16[393,2048]{1,0:T(8,128)(2,1)} %get-tuple-element.54.z_ref, bf16[393,2048]{1,0:T(8,128)(2,1)} %get-tuple-element.55.gz_ref, f32[80,2048]{1,0:T(8,128)} %get-tuple-element.47.y_ref, f32[80,2048]{1,0:T(8,128)} %get-tuple-element.46.gy_ref, ...), custom_call_target="tpu_custom_call" | custom-call | tf_op jit(solution)/shard_map/pallas_call | solution.py:160
  (60 shorter events, 43.7 us)
Async XLA Ops:
  37.9 9.5 %collective-permute-start = (f32[67,67,3]{1,0,2:T(8,128)S(1)}, f32[67,67,3]{1,0,2:T(8,128)S(1)}, u32[]{:S(2)}, u32[]{:S(2)}) collective-permute-start(f32[67,67,3]{1,0,2:T(8,128)S(1)} %copy.17), channel_id=1, source_target_pairs={{0,16},{16,0},{1,17},{17,1},{2,18},{18,2},{3,19},{19,3},{4,20},{20... | collective-permute-start | bytes 161612 | tf_op jit(solution)/shard_map/ppermute | solution.py:24
  52.6 5.7 %collective-permute-start.1 = (f32[3,67,128]{2,1,0:T(8,128)S(1)}, f32[3,67,128]{2,1,0:T(8,128)S(1)}, u32[]{:S(2)}, u32[]{:S(2)}) collective-permute-start(f32[3,67,128]{2,1,0:T(8,128)S(1)} %pad_maximum_fusion.7), channel_id=1, source_target_pairs={{0,1},{1,2},{2,3},{3,0},{4,5},{5,6},{6,7},{7,4},{8,9},{9,10},{10,1... | collective-permute-start | bytes 308744 | tf_op jit(solution)/shard_map/ppermute | solution.py:24
  59.1 4.4 %collective-permute-start.2 = (f32[64,3,128]{2,1,0:T(4,128)S(1)}, f32[64,3,128]{2,1,0:T(4,128)S(1)}, u32[]{:S(2)}, u32[]{:S(2)}) collective-permute-start(f32[64,3,128]{2,1,0:T(4,128)S(1)} %slice.80), channel_id=1, source_target_pairs={{0,4},{4,8},{8,12},{12,0},{1,5},{5,9},{9,13},{13,1},{2,6},{6,10},{... | collective-permute-start | bytes 294920 | tf_op jit(solution)/shard_map/ppermute | solution.py:24
  65.3 28.3 %copy-start.6 = (f32[256,256]{1,0:T(8,128)S(1)}, f32[256,256]{1,0:T(8,128)}, u32[]{:S(2)}) copy-start(f32[256,256]{1,0:T(8,128)} %constant.35.clone) | copy-start | bytes 786436
  95.2 30.3 %copy-start.4 = (f32[512,512]{1,0:T(8,128)S(1)}, f32[512,512]{1,0:T(8,128)}, u32[]{:S(2)}) copy-start(f32[512,512]{1,0:T(8,128)} %constant.36.clone) | copy-start | bytes 3145732
  128.8 51.6 %all-to-all-start.2 = ((f32[2,256,1024]{2,1,0:T(8,128)}), f32[2,256,1024]{2,1,0:T(8,128)S(1)}, u32[]{:S(2)}, u32[]{:S(2)}) async-start(f32[2,256,1024]{2,1,0:T(8,128)} %bitcast.110), calls=%async_computation.2 | async-start | bytes 4194304 | tf_op jit(solution)/shard_map/all_to_all | solution.py:186
  184.3 3.4 copy-start.3
  240.3 2.1 copy-start.2
  275.1 1.0 copy-start.5
  306.5 4.7 %collective-permute-start.3 = (f32[3,64,128]{2,1,0:T(8,128)S(1)}, f32[3,64,128]{2,1,0:T(8,128)S(1)}, u32[]{:S(2)}, u32[]{:S(2)}) collective-permute-start(f32[3,64,128]{2,1,0:T(8,128)S(1)} %slice.82), channel_id=1, source_target_pairs={{0,3},{1,0},{2,1},{3,2},{4,7},{5,4},{6,5},{7,6},{8,11},{9,8},{10,9... | collective-permute-start | bytes 294920 | tf_op jit(solution)/shard_map/ppermute | solution.py:24
  311.2 2.6 collective-permute-start.4
  315.5 3.6 copy-start
  315.5 3.6 copy-start.1
  318.9 9.2 %collective-permute-start.5 = (f32[67,67,3]{1,0,2:T(8,128)}, f32[67,67,3]{1,0,2:T(8,128)}, u32[]{:S(2)}, u32[]{:S(2)}) collective-permute-start(f32[67,67,3]{1,0,2:T(8,128)} %copy.23), channel_id=1, source_target_pairs={{0,16},{16,0},{1,17},{17,1},{2,18},{18,2},{3,19},{19,3},{4,20},{20... | collective-permute-start | bytes 161612 | tf_op jit(solution)/shard_map/ppermute | solution.py:24
where the time goes:
time: 398 us; the launch traced here: 397 us
  blocking collectives  166 us (42%)
  Pallas kernels  76.3 us (19%)
  waiting for transfers between devices  69.9 us (18%)
  other arithmetic  33.7 us (8%)
  local copies, waits for them, and re-layouts  25.5 us (6%)
  matrix products  13.4 us (3%)
  starting transfers between devices  10.8 us (3%)
    all_to_all x5, blocking collectives, exchange(): return lax.all_to_all(data, axes, split_axis=0, concat_axis=0, tiled=True)  166 us
    pallas_call x1, Pallas kernels, gather(): pl.pallas_call(functools.partial(gather_kernel, 256), grid=(pad_x // gath...  53.4 us
    all_to_all x1, waiting for transfers between devices, exchange(): return lax.all_to_all(data, axes, split_axis=0, concat_axis=0, tiled=True)  46.6 us
    ppermute x6, waiting for transfers between devices, from_behind(): return lax.ppermute(value, axis, pairs)  23.3 us
    pallas_call x1, Pallas kernels, spread(): pl.pallas_call(spread_kernel, grid=(span_x // gather_rows,), in_specs=[pl...  22.9 us
    dot_general x6, matrix products, turn(): jnp.dot(jnp.asarray(table, jnp.float32), data, precision=highest, preferr...  13.4 us
    concatenate x1, other arithmetic, gather(): stacked = jnp.concatenate([high, low, high], axis=2)  8.2 us
  transfers between devices with their start and end apart: 7, of which 7 were waited for; matrix products, arithmetic and copies ran while one was open for 2% of the time, Pallas kernels for 0%

commit v1 on v0

v1 whole, which is shorter than its diff:
```python
import functools

import jax
import jax.numpy as jnp
import numpy as np
from jax import lax
from jax.experimental import pallas as pl
from jax.experimental.pallas import tpu as pltpu
from jax.sharding import PartitionSpec as P

GRID = 256
ORDER = 4
LANES = 128
SUBLANES = 8

coulomb = 332.0636
ewald = 0.7
MESH = pl.DeviceIdType.MESH
ROWS_BY_ROWS = (((1,), (1,)), ((), ()))


def round_up(value, unit):
    return -(-value // unit) * unit


def halves(value):
    high = value.astype(jnp.bfloat16)
    low = (value - high.astype(jnp.float32)).astype(jnp.bfloat16)
    return high, low


def constant_halves(value):
    value = np.asarray(value, np.float32)
    high = value.astype(jnp.bfloat16)
    low = (value - high.astype(np.float32)).astype(jnp.bfloat16)
    return jnp.asarray(np.stack([high, low]))


def mm(a, b, contract=(((1,), (0,)), ((), ()))):
    return lax.dot_general(a, b, contract, preferred_element_type=jnp.float32)


class Plan:
    def __init__(self, nz, ny, nx, capacity):
        self.nz, self.ny, self.nx = nz, ny, nx
        self.capacity = capacity
        self.chunks = capacity // LANES
        self.blocks = nz * nx
        self.cells_x = GRID // nx
        self.cells_y = GRID // ny
        self.cells_z = GRID // nz
        self.halo = ORDER - 1
        self.span_x = self.cells_x + self.halo
        self.span_y = self.cells_y + self.halo
        self.window = self.cells_z // nx
        self.octets = self.window // SUBLANES
        self.tiles = -(-self.span_y // nx)
        self.pad_y = self.tiles * nx
        self.rows = self.pad_y * SUBLANES
        self.dests = ny * nx
        self.kept = GRID // 2
        self.width_k = self.kept // self.dests
        self.pad_k = round_up(self.width_k, SUBLANES)
        self.row_k = 2 * self.pad_k
        self.all_y = ny * self.pad_y
        self.pad_x = round_up(self.span_x, SUBLANES)
        self.pack_x = round_up(3 * self.pad_x, LANES)
        assert nz == 2 and self.cells_z == LANES and self.span_x <= LANES

    def angle(self, outputs, inputs):
        return (outputs[:, None] * inputs[None, :] % GRID) * (2.0 * np.pi / GRID)

    def index_kx(self):
        place = np.arange(self.pad_k)
        index = np.arange(self.dests)[:, None] * self.width_k + np.minimum(place, self.width_k - 1)[None, :]
        return index.reshape(-1), np.tile(place < self.width_k, self.dests)

    def pairs(self, cosine, sine):
        shape = (self.dests, 1, self.pad_k, -1)
        both = np.concatenate([cosine.reshape(shape), sine.reshape(shape)], axis=1)
        return both.reshape(self.dests * self.row_k, -1)

    def x_forward(self):
        local = np.arange(LANES)
        cells = (np.arange(self.nx)[:, None] * self.cells_x + local[None, :]).reshape(-1)
        used = np.tile(local < self.span_x, self.nx)
        index, kept = self.index_kx()
        angle = self.angle(index, cells)
        mask = kept[:, None] * used[None, :]
        return constant_halves(self.pairs(np.cos(angle) * mask, -np.sin(angle) * mask))

    def x_inverse(self):
        lane = np.arange(self.pack_x)
        local = lane % self.pad_x
        cells = (np.arange(self.nx)[:, None] * self.cells_x + local[None, :]).reshape(-1)
        used = np.tile((local < self.span_x) & (lane < 3 * self.pad_x), self.nx)
        index, kept = self.index_kx()
        angle = self.angle(index, cells)
        mask = (kept * np.where(index > 0, 2.0, 1.0))[:, None] * used[None, :]
        return constant_halves(self.pairs(np.cos(angle) * mask, -np.sin(angle) * mask))

    def z_tables(self):
        cells = np.arange(self.cells_z)
        tables = []
        for parity in range(self.nz):
            angle = self.angle(self.nz * cells + parity, cells)
            forward = np.concatenate([np.cos(angle).T, np.sin(angle).T], axis=1)
            inverse = np.concatenate([np.cos(angle), np.sin(angle)], axis=1)
            tables += [constant_halves(forward), constant_halves(inverse)]
        return jnp.stack(tables).reshape(self.nz, 2, 2, self.cells_z, 2 * self.cells_z)

    def y_tables(self):
        local = np.arange(self.pad_y)
        cells = (np.arange(self.ny)[:, None] * self.cells_y + local[None, :]).reshape(-1)
        used = np.tile(local < self.span_y, self.ny)
        angle = self.angle(np.arange(GRID), cells)
        cosine, sine = np.cos(angle) * used[None, :], np.sin(angle) * used[None, :]
        forward = constant_halves(np.concatenate([cosine, sine], axis=1))
        inverse = constant_halves(np.concatenate([cosine.T, sine.T], axis=1))
        return forward, inverse

    def green_lines(self):
        index = np.arange(GRID)
        signed = np.where(2 * index < GRID, index, index - GRID)
        square = (signed * signed).astype(np.float32)
        bspline = 36.0 / (4.0 + 2.0 * np.cos(index * (2.0 * np.pi / GRID))) ** 2
        bspline = np.where(2 * index == GRID, 0.0, bspline).astype(np.float32)
        line_x = np.stack([square, bspline])[:, : self.kept]
        line_y = np.stack([square, bspline])[:, :, None]
        line_z = np.stack([square, bspline]).reshape(2, 1, self.cells_z, self.nz)
        line_z = line_z.transpose(3, 0, 1, 2)
        return jnp.asarray(line_x), jnp.asarray(line_y), jnp.asarray(line_z)


def exchange_kernel(axes, sizes, same, src_ref, out_ref, send_sems, recv_sems, local_sem):
    count = int(np.prod(sizes))
    me = 0
    for axis, size in zip(axes, sizes):
        me = me * size + lax.axis_index(axis)

    def place(member):
        where = {}
        for axis, size in reversed(list(zip(axes, sizes))):
            where[axis] = lax.rem(member, size)
            member = member // size
        return where

    barrier = pltpu.get_barrier_semaphore()
    for step in range(1, count):
        pl.semaphore_signal(
            barrier, inc=1, device_id=place(lax.rem(me + step, count)), device_id_type=MESH
        )
    pl.semaphore_wait(barrier, count - 1)
    copies = []
    for step in range(1, count):
        peer = lax.rem(me + step, count)
        copy = pltpu.make_async_remote_copy(
            src_ref=src_ref if same else src_ref.at[peer],
            dst_ref=out_ref.at[me],
            send_sem=send_sems.at[step],
            recv_sem=recv_sems.at[step],
            device_id=place(peer),
            device_id_type=MESH,
        )
        copy.start()
        copies.append(copy)
    own = pltpu.make_async_copy(src_ref if same else src_ref.at[me], out_ref.at[me], local_sem)
    own.start()
    own.wait()
    for copy in copies:
        copy.wait()


def exchange(data, axes, collective_id, same=False):
    sizes = [lax.axis_size(axis) for axis in axes]
    count = int(np.prod(sizes))
    shape = ((count,) if same else ()) + data.shape
    return pl.pallas_call(
        functools.partial(exchange_kernel, axes, sizes, same),
        in_specs=[pl.BlockSpec(memory_space=pltpu.VMEM)],
        out_specs=pl.BlockSpec(memory_space=pltpu.VMEM),
        out_shape=jax.ShapeDtypeStruct(shape, data.dtype),
        scratch_shapes=[
            pltpu.SemaphoreType.DMA((count,)),
            pltpu.SemaphoreType.DMA((count,)),
            pltpu.SemaphoreType.DMA,
        ],
        compiler_params=pltpu.CompilerParams(
            collective_id=collective_id, has_side_effects=True
        ),
    )(data)


def spline_rows(frac):
    rest = 1.0 - frac
    square = frac * frac
    cube = square * frac
    weights = [
        rest * rest * rest / 6.0,
        (3.0 * cube - 6.0 * square + 4.0) / 6.0,
        (-3.0 * cube + 3.0 * square + 3.0 * frac + 1.0) / 6.0,
        cube / 6.0,
    ]
    slopes = [
        -0.5 * rest * rest,
        1.5 * square - 2.0 * frac,
        -1.5 * square + frac + 0.5,
        0.5 * square,
    ]
    return weights, slopes


def placed(offset, values, dim):
    total = jnp.zeros(offset.shape, jnp.float32)
    for k in range(ORDER):
        total = jnp.where(offset == float(k), values[k][dim : dim + 1], total)
    return total


def offsets(rows, lowest):
    return lax.broadcasted_iota(jnp.int32, (rows, LANES), 0).astype(jnp.float32) - lowest


def fold_sign(parity, part):
    return (1 - 2 * lax.rem(parity * part, 2)).astype(jnp.float32)


def over_chunks(plan, bounds_ref, work):
    first = lax.axis_index("gx") * plan.window

    def step(i, carry):
        low = bounds_ref[0, i]
        high = bounds_ref[1, i] + plan.halo

        def meets(start, length):
            inside = (low <= start + length - 1) & (high >= start)
            return inside | (high >= plan.cells_z + start)

        @pl.when(meets(first, plan.window))
        def _():
            work(i // plan.chunks, lax.rem(i, plan.chunks), meets)

        return carry

    lax.fori_loop(0, plan.blocks * plan.chunks, step, 0)


def z_rows(plan, values, lowest, parity):
    offset = offsets(plan.window, lowest - (lax.axis_index("gx") * plan.window).astype(jnp.float32))
    wrapped = placed(offset + float(plan.cells_z), values, 2)
    return placed(offset, values, 2) + fold_sign(parity, 1) * wrapped


def spread_kernel(plan, bounds_ref, atoms_ref, dft_ref, out_ref, grid_ref, y_ref, z_ref, x_ref, a_ref):
    parity = lax.axis_index("gz")
    first = lax.axis_index("gx") * plan.window
    grid_ref[...] = jnp.zeros_like(grid_ref)
    x_ref[...] = jnp.zeros_like(x_ref)

    def work(block, chunk, meets):
        atoms = atoms_ref[block, :, pl.ds(pl.multiple_of(chunk * LANES, LANES), LANES)]
        weights, _ = spline_rows(atoms[0:3])
        sign = fold_sign(parity, block // plan.nx)
        rows_x = placed(offsets(plan.pad_x, atoms[4:5]), weights, 0)
        y_ref[...] = placed(offsets(plan.pad_y, atoms[5:6]), weights, 1)
        z_ref[...] = z_rows(plan, weights, atoms[6:7], parity) * (atoms[3:4] * sign)
        rows_x = jnp.concatenate(
            [rows_x, jnp.zeros((LANES - plan.pad_x, LANES), jnp.float32)], axis=0
        )
        high, low = halves(rows_x)
        x_ref[:LANES, :LANES] = high
        x_ref[:LANES, LANES:] = high
        x_ref[LANES:, :LANES] = low
        place = pl.multiple_of(lax.rem(block, plan.nx) * LANES, LANES)
        for octet in range(plan.octets):

            @pl.when(meets(first + octet * SUBLANES, SUBLANES))
            def _():
                line = z_ref[octet * SUBLANES : (octet + 1) * SUBLANES]
                for y in range(0, plan.pad_y, 2):
                    pair = jnp.concatenate([y_ref[y : y + 1] * line, y_ref[y + 1 : y + 2] * line], axis=0)
                    high, low = halves(pair)
                    a_ref[y * SUBLANES : (y + 2) * SUBLANES, :LANES] = high
                    a_ref[y * SUBLANES : (y + 2) * SUBLANES, LANES:] = low
                product = mm(a_ref[...], x_ref[...], ROWS_BY_ROWS)
                grid_ref[octet, :, pl.ds(place, LANES)] += product[:, :LANES] + product[:, LANES:]

    over_chunks(plan, bounds_ref, work)

    def transform(tile, carry):
        pieces = []
        for part in range(plan.nx):
            row = pl.multiple_of((tile * plan.nx + part) * SUBLANES, SUBLANES)
            for octet in range(plan.octets):
                pieces.append(grid_ref[octet, pl.ds(row, SUBLANES), :])
        high, low = halves(jnp.concatenate(pieces, axis=0))
        first_pass = mm(dft_ref[0], jnp.concatenate([high, low], axis=0), ROWS_BY_ROWS)
        second_pass = mm(dft_ref[1], high, ROWS_BY_ROWS)
        total = first_pass[:, :LANES] + (first_pass[:, LANES:] + second_pass)
        here = pl.ds(pl.multiple_of(tile * LANES, LANES), LANES)
        out_ref[:, :, here] = total.reshape(plan.dests, plan.row_k, LANES)
        return carry

    lax.fori_loop(0, plan.tiles, transform, 0)


def regroup(plan, values):
    shape = values[0].shape
    group = lax.broadcasted_iota(jnp.int32, shape, 1) // plan.window
    moved = []
    for step in range(plan.nx):
        mixed = values[step % plan.nx]
        for part in range(1, plan.nx):
            mixed = jnp.where(group == part, values[(part + step) % plan.nx], mixed)
        moved.append(pltpu.roll(mixed, step * plan.window, 1) if step else mixed)
    results = []
    for part in range(plan.nx):
        result = moved[(-part) % plan.nx]
        for other in range(1, plan.nx):
            result = jnp.where(group == other, moved[(other - part) % plan.nx], result)
        results.append(result)
    return results


def middle_kernel(plan, in_ref, z_table_ref, y_forward_ref, y_inverse_ref, line_x_ref, line_y_ref, line_z_ref, out_ref, u_ref, o_ref, mid_ref):
    parity = lax.axis_index("gz")
    device = lax.axis_index("gy") * plan.nx + lax.axis_index("gx")
    row_k, pad_k = plan.row_k, plan.pad_k
    shape = (plan.pad_y, 2, pad_k, 2 * LANES)

    def z_transform(direction):
        high = z_table_ref[parity, direction, 0]
        both = jnp.concatenate([high, high], axis=0)
        total = mm(u_ref[...], both) + mm(u_ref[:, :LANES], z_table_ref[parity, direction, 1])
        return total.reshape(shape)

    def forward(gy, carry):
        def tile_step(tile, carry):
            here = pl.ds(pl.multiple_of(tile * LANES, LANES), LANES)
            values = [in_ref[gy * plan.nx + gx, :, here] for gx in range(plan.nx)]
            for part, value in enumerate(regroup(plan, values)):
                rows = pl.ds(pl.multiple_of((tile * plan.nx + part) * row_k, row_k), row_k)
                high, low = halves(value)
                u_ref[rows, :LANES] = high
                u_ref[rows, LANES:] = low
            return carry

        lax.fori_loop(0, plan.tiles, tile_step, 0)
        total = z_transform(0)
        real, imag = total[:, 0], total[:, 1]
        rows = pl.ds(pl.multiple_of(gy * (plan.pad_y * pad_k), pad_k), plan.pad_y * pad_k)
        mid_ref[0, rows, :] = (real[..., :LANES] + imag[..., LANES:]).reshape(-1, LANES)
        mid_ref[1, rows, :] = (imag[..., :LANES] - real[..., LANES:]).reshape(-1, LANES)
        return carry

    lax.fori_loop(0, plan.ny, forward, 0)

    def column(j, carry):
        lines = pl.ds(j, plan.all_y, stride=pad_k)
        real = mid_ref[0, lines, :]
        imag = mid_ref[1, lines, :]
        stacked = jnp.concatenate(
            [jnp.concatenate([real, imag], axis=1), jnp.concatenate([imag, -real], axis=1)], axis=0
        )
        high, low = halves(stacked)
        spectrum = mm(y_forward_ref[0], high) + (mm(y_forward_ref[0], low) + mm(y_forward_ref[1], high))
        kx = device * plan.width_k + j
        square = (line_y_ref[0] + line_z_ref[parity, 0]) + line_x_ref[0, kx]
        factor = (line_y_ref[1] * line_z_ref[parity, 1]) * line_x_ref[1, kx]
        green = jnp.where(
            square > 0.0,
            coulomb
            * jnp.exp(square * (-np.pi**2 / (ewald * ewald * GRID * GRID)))
            * factor
            / (np.pi * GRID * jnp.maximum(square, 1.0)),
            0.0,
        )
        real = spectrum[:, :LANES] * green
        imag = spectrum[:, LANES:] * green
        stacked = jnp.concatenate(
            [jnp.concatenate([real, imag], axis=1), jnp.concatenate([-imag, real], axis=1)], axis=0
        )
        high, low = halves(stacked)
        result = mm(y_inverse_ref[0], high) + (mm(y_inverse_ref[0], low) + mm(y_inverse_ref[1], high))
        mid_ref[0, lines, :] = result[:, :LANES]
        mid_ref[1, lines, :] = result[:, LANES:]
        return carry

    lax.fori_loop(0, plan.width_k, column, 0)

    def backward(gy, carry):
        rows = pl.ds(pl.multiple_of(gy * (plan.pad_y * pad_k), pad_k), plan.pad_y * pad_k)
        real = mid_ref[0, rows, :].reshape(plan.pad_y, pad_k, LANES)
        imag = mid_ref[1, rows, :].reshape(plan.pad_y, pad_k, LANES)
        high, low = halves(jnp.concatenate([real, imag], axis=1).reshape(-1, LANES))
        u_ref[:, :LANES] = high
        u_ref[:, LANES:] = low
        total = z_transform(1)
        real, imag = total[:, 0], total[:, 1]
        result = jnp.concatenate(
            [real[..., :LANES] - imag[..., LANES:], imag[..., :LANES] + real[..., LANES:]], axis=1
        )
        o_ref[...] = result.reshape(-1, LANES)

        def tile_step(tile, carry):
            values = []
            for part in range(plan.nx):
                rows = pl.ds(pl.multiple_of((tile * plan.nx + part) * row_k, row_k), row_k)
                values.append(o_ref[rows, :])
            here = pl.ds(pl.multiple_of(tile * LANES, LANES), LANES)
            for gx, value in enumerate(regroup(plan, values)):
                out_ref[gy * plan.nx + gx, :, here] = value
            return carry

        lax.fori_loop(0, plan.tiles, tile_step, 0)
        return carry

    lax.fori_loop(0, plan.ny, backward, 0)


def gather_kernel(plan, bounds_ref, atoms_ref, in_ref, dft_ref, out_ref, pot_ref, y_ref, z_ref, x_ref, p_ref, sum_ref):
    parity = lax.axis_index("gz")
    first = lax.axis_index("gx") * plan.window
    out_ref[...] = jnp.zeros_like(out_ref)
    x_ref[...] = jnp.zeros_like(x_ref)
    pack = plan.pack_x

    def transform(tile, carry):
        here = pl.ds(pl.multiple_of(tile * LANES, LANES), LANES)
        lines = in_ref[:, :, here].reshape(plan.dests * plan.row_k, LANES)
        high, low = halves(lines.T)
        first_pass = mm(jnp.concatenate([high, low], axis=0), dft_ref[0])
        value = first_pass[:LANES] + (first_pass[LANES:] + mm(high, dft_ref[1]))
        lane = lax.rem(lax.broadcasted_iota(jnp.int32, value.shape, 1), pack)
        rest = value - value.astype(jnp.bfloat16).astype(jnp.float32)
        value = jnp.where((lane >= plan.pad_x) & (lane < 2 * plan.pad_x), rest, value)
        for octet in range(plan.octets):
            for part in range(0, plan.nx, 2):
                pieces = []
                for other in range(2):
                    row = (part + other) * plan.window + octet * SUBLANES
                    pieces.append(value[row : row + SUBLANES])
                row = pl.multiple_of((tile * plan.nx + part) * SUBLANES, 2 * SUBLANES)
                pot_ref[octet, pl.ds(row, 2 * SUBLANES), :] = jnp.concatenate(pieces, axis=0).astype(jnp.bfloat16)
        return carry

    lax.fori_loop(0, plan.tiles, transform, 0)

    def work(block, chunk, meets):
        atoms = atoms_ref[block, :, pl.ds(pl.multiple_of(chunk * LANES, LANES), LANES)]
        weights, slopes = spline_rows(atoms[0:3])
        sign = fold_sign(parity, block // plan.nx)
        offset = offsets(plan.pad_x, atoms[4:5])
        table = jnp.concatenate([placed(offset, weights, 0), placed(offset, slopes, 0)], axis=1)
        high = table.astype(jnp.bfloat16).astype(jnp.float32)
        unused = jnp.zeros((pack - 3 * plan.pad_x, 2 * LANES), jnp.float32)
        x_ref[...] = jnp.concatenate([high, high, table - high, unused], axis=0).astype(jnp.bfloat16)
        offset = offsets(plan.pad_y, atoms[5:6])
        y_ref[0] = placed(offset, weights, 1)
        y_ref[1] = placed(offset, slopes, 1)
        z_ref[0] = z_rows(plan, weights, atoms[6:7], parity) * sign
        z_ref[1] = z_rows(plan, slopes, atoms[6:7], parity) * sign
        sum_ref[...] = jnp.zeros_like(sum_ref)
        place = pl.multiple_of(lax.rem(block, plan.nx) * pack, LANES)
        for octet in range(plan.octets):

            @pl.when(meets(first + octet * SUBLANES, SUBLANES))
            def _():
                p_ref[...] = mm(pot_ref[octet, :, pl.ds(place, pack)], x_ref[...])
                total_x = jnp.zeros((SUBLANES, LANES), jnp.float32)
                total_y = jnp.zeros((SUBLANES, LANES), jnp.float32)
                total_z = jnp.zeros((SUBLANES, LANES), jnp.float32)
                for y in range(plan.pad_y):
                    rows = slice(y * SUBLANES, (y + 1) * SUBLANES)
                    plain = p_ref[rows, :LANES]
                    weight = y_ref[0, y : y + 1]
                    total_x += weight * p_ref[rows, LANES:]
                    total_y += y_ref[1, y : y + 1] * plain
                    total_z += weight * plain
                lines = slice(octet * SUBLANES, (octet + 1) * SUBLANES)
                weight = z_ref[0, lines]
                sum_ref[0] += weight * total_x
                sum_ref[1] += weight * total_y
                sum_ref[2] += z_ref[1, lines] * total_z

        for dim in range(3):
            row = jnp.sum(sum_ref[dim], axis=0, keepdims=True)
            out_ref[block, pl.ds(dim * plan.chunks + chunk, 1), :] = row

    over_chunks(plan, bounds_ref, work)


def vmem_call(kernel, out_shape, scratch_shapes, smem=()):
    def call(*operands):
        specs = [
            pl.BlockSpec(memory_space=pltpu.SMEM if i in smem else pltpu.VMEM)
            for i in range(len(operands))
        ]
        return pl.pallas_call(
            kernel,
            in_specs=specs,
            out_specs=pl.BlockSpec(memory_space=pltpu.VMEM),
            out_shape=out_shape,
            scratch_shapes=scratch_shapes,
            compiler_params=pltpu.CompilerParams(vmem_limit_bytes=50 * 2**20),
        )(*operands)

    return call


def per_device(charges, fractions, base_cells, counts):
    capacity = charges.shape[0]
    plan = Plan(lax.axis_size("gz"), lax.axis_size("gy"), lax.axis_size("gx"), capacity)
    f32, bf16 = jnp.float32, jnp.bfloat16
    slot = jnp.arange(capacity, dtype=jnp.int32)
    live = slot < counts.reshape(())
    charge = jnp.where(live, charges, jnp.zeros_like(charges))
    local_x = (base_cells[0] - lax.axis_index("gx") * plan.cells_x).astype(f32)
    local_y = (base_cells[1] - lax.axis_index("gy") * plan.cells_y).astype(f32)
    key = jnp.where(live, base_cells[2] - lax.axis_index("gz") * plan.cells_z, plan.cells_z)
    key, slot, t_x, t_y, t_z, charge, local_x, local_y = lax.sort(
        [key, slot, fractions[0], fractions[1], fractions[2], charge, local_x, local_y],
        num_keys=1,
        is_stable=False,
    )
    atoms = jnp.stack([t_x, t_y, t_z, charge, local_x, local_y, key.astype(f32), jnp.zeros_like(t_x)])
    atoms = exchange(atoms, ("gz", "gx"), 0, same=True)
    low = atoms[:, 6, ::LANES]
    high = jnp.minimum(atoms[:, 6, LANES - 1 :: LANES], plan.cells_z - 1.0)
    high = jnp.where(low < plan.cells_z, high, -2.0 * plan.halo)
    bounds = jnp.stack([low, high]).astype(jnp.int32).reshape(2, -1)

    lanes = plan.tiles * LANES
    half_shape = jax.ShapeDtypeStruct((plan.dests, plan.row_k, lanes), f32)
    data = vmem_call(
        functools.partial(spread_kernel, plan),
        half_shape,
        [
            pltpu.VMEM((plan.octets, plan.rows, plan.nx * LANES), f32),
            pltpu.VMEM((plan.pad_y, LANES), f32),
            pltpu.VMEM((plan.window, LANES), f32),
            pltpu.VMEM((2 * LANES, 2 * LANES), bf16),
            pltpu.VMEM((plan.rows, 2 * LANES), bf16),
        ],
        smem=(0,),
    )(bounds, atoms, plan.x_forward())
    data = exchange(data, ("gy", "gx"), 1)
    y_forward, y_inverse = plan.y_tables()
    line_x, line_y, line_z = plan.green_lines()
    data = vmem_call(
        functools.partial(middle_kernel, plan),
        half_shape,
        [
            pltpu.VMEM((plan.pad_y * plan.row_k, 2 * LANES), bf16),
            pltpu.VMEM((plan.pad_y * plan.row_k, LANES), f32),
            pltpu.VMEM((2, plan.all_y * plan.pad_k, LANES), f32),
        ],
        smem=(4,),
    )(data, plan.z_tables(), y_forward, y_inverse, line_x, line_y, line_z)
    data = exchange(data, ("gy", "gx"), 2)
    parts = vmem_call(
        functools.partial(gather_kernel, plan),
        jax.ShapeDtypeStruct((plan.blocks, 3 * plan.chunks, LANES), f32),
        [
            pltpu.VMEM((plan.octets, plan.rows, plan.nx * plan.pack_x), bf16),
            pltpu.VMEM((2, plan.pad_y, LANES), f32),
            pltpu.VMEM((2, plan.window, LANES), f32),
            pltpu.VMEM((plan.pack_x, 2 * LANES), bf16),
            pltpu.VMEM((plan.rows, 2 * LANES), f32),
            pltpu.VMEM((3, SUBLANES, LANES), f32),
        ],
        smem=(0,),
    )(bounds, atoms, data, plan.x_inverse())
    parts = exchange(parts, ("gz", "gx"), 3)
    forces = -charge[None, :] * jnp.sum(parts, axis=0).reshape(3, capacity)
    result = lax.sort([slot, forces[0], forces[1], forces[2]], num_keys=1, is_stable=False)
    return jnp.stack(result[1:])


def solution(mesh):
    in_specs = (
        P(("gz", "gy", "gx")),
        P(None, ("gz", "gy", "gx")),
        P(None, ("gz", "gy", "gx")),
        P("gz", "gy", "gx"),
    )
    out_specs = P(None, ("gz", "gy", "gx"))
    return jax.shard_map(
        per_device, mesh=mesh, in_specs=in_specs, out_specs=out_specs, check_vma=False
    )
```

time: 398 us -> 216 us (0.54)
  blocking collectives: 166 us -> 0 us
  Pallas kernels: 76.3 us -> 189 us
  waiting for transfers between devices: 69.9 us -> 0 us
  other arithmetic: 33.7 us -> 13.1 us
  local copies, waits for them, and re-layouts: 25.5 us -> 10.4 us
  matrix products: 13.4 us -> 0 us
  starting transfers between devices: 10.8 us -> 0 us
    all_to_all x5 -> x0, blocking collectives: 166 us -> none  [exchange(): return lax.all_to_all(data, axes, split_axis=0, concat_axis=0, tiled=True)]
    pallas_call x2 -> x7, Pallas kernels: 76.3 us -> 189 us  [the longest x4 99.9 us: exchange(): pl.pallas_call(functools.partial(exchange_kernel, axes, sizes, same), in_...]
    all_to_all x1 -> x0, waiting for transfers between devices: 46.6 us -> none  [exchange(): return lax.all_to_all(data, axes, split_axis=0, concat_axis=0, tiled=True)]
    ppermute x6 -> x0, waiting for transfers between devices: 23.3 us -> none  [from_behind(): return lax.ppermute(value, axis, pairs)]
    concatenate x6 -> x0, other arithmetic: 14.5 us -> none  [the longest x1 8.2 us: gather(): stacked = jnp.concatenate([high, low, high], axis=2)]
    dot_general x6 -> x0, matrix products: 13.4 us -> none  [turn(): jnp.dot(jnp.asarray(table, jnp.float32), data, precision=highest, preferr...]
    sort x0 -> x2, other arithmetic: none -> 9.21 us  [the longest x1 4.89 us: per_device(): lax.sort([slot, forces[0], forces[1], forces[2]], num_keys=1, is_stable=F...]
    add x6 -> x0, other arithmetic: 8.03 us -> none  [the longest x2 5.1 us: place_rows(): placed + jnp.where(offset == order_index, values[order_index][None, :], 0.0)]
  transfers between devices with their start and end apart: 7 -> 0, of which waited for: 7 -> 0; matrix products, arithmetic and copies ran while one was open for 2% -> 0% of each run, Pallas kernels for 0% -> 0%
where the time goes in v1:
time: 216 us; the launch traced here: 214 us
  Pallas kernels  189 us (88%)
  other arithmetic  13.1 us (6%)
  local copies, waits for them, and re-layouts  10.4 us (5%)
    pallas_call x4, Pallas kernels, exchange(): pl.pallas_call(functools.partial(exchange_kernel, axes, sizes, same), in_...  99.9 us
    pallas_call x3, Pallas kernels, call(): pl.pallas_call(kernel, in_specs=specs, out_specs=pl.BlockSpec(memory_spac...  89.6 us
    unnamed x26, local copies, waits for them, and re-layouts  5.75 us
    sort x1, other arithmetic, per_device(): lax.sort([slot, forces[0], forces[1], forces[2]], num_keys=1, is_stable=F...  4.89 us
    sort x1, other arithmetic, per_device(): lax.sort([key, slot, fractions[0], fractions[1], fractions[2], charge, lo...  4.33 us

profile of v1, /device:TPU:0, one launch (start us, length us, event | category | flops | bytes accessed | tf_op | source)
XLA Modules:
  0.0 213.8 jit_solution(12188897919662953824)
XLA Ops:
  0.7 0.7 fusion
  1.4 0.9 subtract_convert_fusion
  2.3 0.9 fusion.3
  3.2 4.3 %sort.78 = (s32[2048]{0:T(1024)S(1)}, s32[2048]{0:T(1024)S(1)}, f32[2048]{0:T(1024)S(1)}, f32[2048]{0:T(1024)S(1)}, f32[2048]{0:T(1024)S(1)}, /*index=5*/f32[2048]{0:T(1024)S(1)}, f32[2048]{0:T(1024)S(1)}, f32[2048]{0:T(1024)S(1)}) sort(s32[2048]{0:T(1024)S(1)} %fusion.1, s32[2048]{0:T(1024)S(1)} %iota.6, f32[2048]{0:T(1024)S(1)} %bitcast.31, ...), dimensions={0}, to_apply=%region_0.1 | sort | flops 22528 | bytes 131072 | tf_op jit(solution)/shard_map/sort | solution.py:521
  7.5 0.7 stack.61.src_ref
  8.2 16.8 %shard_map.145.atoms_ref = f32[8,8,2048]{2,1,0:T(8,128)} custom-call(f32[8,2048]{1,0:T(8,128)} %stack.61.src_ref), custom_call_target="tpu_custom_call" | custom-call | tf_op jit(solution)/shard_map/pallas_call | solution.py:178
  25.1 1.1 slice.40
  26.3 1.1 slice.39
  27.5 0.5 broadcast.39
  28.0 0.7 reduce.7
  28.8 1.0 copy-done.2
  29.8 1.0 copy-done.9
  30.9 29.9 %shard_map.146.src_ref = f32[16,16,2176]{2,1,0:T(8,128)S(1)} custom-call(s32[2,128]{1,0:T(2,128)S(1)} %maximum_convert_fusion.bounds_ref, f32[8,8,2048]{2,1,0:T(8,128)S(1)} %copy-done.2, bf16[2,256,512]{2,1,0:T(8,128)(2,1)S(1)} %copy-done.9), custom_call_target="tpu_custom_call" | custom-call | tf_op jit(solution)/shard_map/pallas_call | solution.py:499
  60.7 1.4 copy-done.1
  62.1 38.2 %shard_map.147.in_ref = f32[16,16,2176]{2,1,0:T(8,128)} custom-call(f32[16,16,2176]{2,1,0:T(8,128)} %copy-done.1), custom_call_target="tpu_custom_call" | custom-call | tf_op jit(solution)/shard_map/pallas_call | solution.py:178
  100.3 27.8 %shard_map.148.src_ref = f32[16,16,2176]{2,1,0:T(8,128)} custom-call(f32[16,16,2176]{2,1,0:T(8,128)} %shard_map.147.in_ref, bf16[2,2,2,128,256]{4,3,2,1,0:T(8,128)(2,1)S(1)} %copy-done.8, bf16[2,256,544]{2,1,0:T(8,128)(2,1)S(1)} %copy-done.6, bf16[2,272,512]{2,1,0:T(8,128)(2,1)S(1)} %copy-done.7, f32[2,128]{1,0:T(2,128)S(1)} %copy-done.12, ...), custom_call_target="tpu_custom_call" | custom-call | tf_op jit(solution)/shard_map/pallas_call | solution.py:499
  128.2 36.1 %shard_map.149.in_ref = f32[16,16,2176]{2,1,0:T(8,128)} custom-call(f32[16,16,2176]{2,1,0:T(8,128)} %shard_map.148.src_ref), custom_call_target="tpu_custom_call" | custom-call | tf_op jit(solution)/shard_map/pallas_call | solution.py:178
  164.3 1.6 copy-done
  165.9 31.9 %shard_map.150.src_ref = f32[8,48,128]{2,1,0:T(8,128)S(1)} custom-call(s32[2,128]{1,0:T(2,128)S(1)} %maximum_convert_fusion.bounds_ref, f32[8,8,2048]{2,1,0:T(8,128)S(1)} %copy-done.3, f32[16,16,2176]{2,1,0:T(8,128)S(1)} %copy-done, bf16[2,256,1024]{2,1,0:T(8,128)(2,1)S(1)} %copy-done.4), custom_call_target="tpu_custom_call" | custom-call | tf_op jit(solution)/shard_map/pallas_call | solution.py:499
  197.9 0.7 copy-done.5
  198.5 8.8 %shard_map.151 = f32[8,48,128]{2,1,0:T(8,128)} custom-call(f32[8,48,128]{2,1,0:T(8,128)} %copy-done.5), custom_call_target="tpu_custom_call" | custom-call | tf_op jit(solution)/shard_map/pallas_call | solution.py:178
  207.3 0.9 reduce_sum.9
  208.3 4.9 %sort.79 = (s32[2048]{0:T(1024)}, f32[2048]{0:T(1024)S(1)}, f32[2048]{0:T(1024)S(1)}, f32[2048]{0:T(1024)S(1)}) sort(s32[2048]{0:T(1024)S(1)} %get-tuple-element.16, f32[2048]{0:T(1024)S(1)} %bitcast.29, f32[2048]{0:T(1024)S(1)} %bitcast.28, f32[2048]{0:T(1024)S(1)} %bitcast.27), dimensions={0}, to_apply=%region_2.3 | sort | flops 22528 | bytes 65536 | tf_op jit(solution)/shard_map/sort | solution.py:576
  213.2 0.6 pad_maximum_fusion
  (34 shorter events, 0.3 us)
Async XLA Ops:
  28.8 1.0 copy-start.2
  29.8 1.0 copy-start.9
  60.7 1.4 copy-start.1
  62.1 38.2 %copy-start.6 = (bf16[2,256,544]{2,1,0:T(8,128)(2,1)S(1)}, bf16[2,256,544]{2,1,0:T(8,128)(2,1)}, u32[]{:S(2)}) copy-start(bf16[2,256,544]{2,1,0:T(8,128)(2,1)} %constant.48.clone.y_forward_ref) | copy-start | bytes 1671172
  62.1 38.2 %copy-start.7 = (bf16[2,272,512]{2,1,0:T(8,128)(2,1)S(1)}, bf16[2,272,512]{2,1,0:T(8,128)(2,1)}, u32[]{:S(2)}) copy-start(bf16[2,272,512]{2,1,0:T(8,128)(2,1)} %constant.49.clone.y_inverse_ref) | copy-start | bytes 1671172
  62.1 38.2 %copy-start.8 = (bf16[2,2,2,128,256]{4,3,2,1,0:T(8,128)(2,1)S(1)}, bf16[2,2,2,128,256]{4,3,2,1,0:T(8,128)(2,1)}, u32[]{:S(2)}) copy-start(bf16[2,2,2,128,256]{4,3,2,1,0:T(8,128)(2,1)} %constant.62.z_table_ref) | copy-start | bytes 1572868
  62.1 38.2 %copy-start.10 = (f32[2,256,1]{2,1,0:T(8,128)S(1)}, f32[2,256,1]{2,1,0:T(8,128)}, u32[]{:S(2)}) copy-start(f32[2,256,1]{2,1,0:T(8,128)} %constant.51.clone.line_y_ref) | copy-start | bytes 6148
  62.1 38.2 %copy-start.11 = (f32[2,2,1,128]{3,2,1,0:T(1,128)S(1)}, f32[2,2,1,128]{3,2,1,0:T(1,128)}, u32[]{:S(2)}) copy-start(f32[2,2,1,128]{3,2,1,0:T(1,128)} %constant.52.clone.line_z_ref) | copy-start | bytes 6148
  62.1 38.2 %copy-start.12 = (f32[2,128]{1,0:T(2,128)S(1)}, f32[2,128]{1,0:T(2,128)}, u32[]{:S(2)}) copy-start(f32[2,128]{1,0:T(2,128)} %constant.50.clone.line_x_ref) | copy-start | bytes 3076
  128.1 36.1 %copy-start.3 = (f32[8,8,2048]{2,1,0:T(8,128)S(1)}, f32[8,8,2048]{2,1,0:T(8,128)}, u32[]{:S(2)}) copy-start(f32[8,8,2048]{2,1,0:T(8,128)} %shard_map.145.atoms_ref) | copy-start | bytes 1572868
  128.2 36.1 %copy-start.4 = (bf16[2,256,1024]{2,1,0:T(8,128)(2,1)S(1)}, bf16[2,256,1024]{2,1,0:T(8,128)(2,1)}, u32[]{:S(2)}) copy-start(bf16[2,256,1024]{2,1,0:T(8,128)(2,1)} %constant.56.clone.dft_ref) | copy-start | bytes 3145732
  164.3 1.6 copy-start
  197.8 0.7 copy-start.5

commit v2 on v1

v2 whole, which is shorter than its diff:
```python
import functools

import jax
import jax.numpy as jnp
import numpy as np
from jax import lax
from jax.experimental import pallas as pl
from jax.experimental.pallas import tpu as pltpu
from jax.sharding import PartitionSpec as P

GRID = 256
ORDER = 4
LANES = 128
SUBLANES = 8

coulomb = 332.0636
ewald = 0.7
MESH = pl.DeviceIdType.MESH
ROWS_BY_ROWS = (((1,), (1,)), ((), ()))


def round_up(value, unit):
    return -(-value // unit) * unit


def halves(value):
    high = value.astype(jnp.bfloat16)
    low = (value - high.astype(jnp.float32)).astype(jnp.bfloat16)
    return high, low


def constant_halves(value):
    value = np.asarray(value, np.float32)
    high = value.astype(jnp.bfloat16)
    low = (value - high.astype(np.float32)).astype(jnp.bfloat16)
    return jnp.asarray(np.stack([high, low]))


def mm(a, b, contract=(((1,), (0,)), ((), ()))):
    return lax.dot_general(a, b, contract, preferred_element_type=jnp.float32)


class Plan:
    def __init__(self, nz, ny, nx, capacity):
        self.nz, self.ny, self.nx = nz, ny, nx
        self.capacity = capacity
        self.chunks = capacity // LANES
        self.blocks = nz * nx
        self.cells_x = GRID // nx
        self.cells_y = GRID // ny
        self.cells_z = GRID // nz
        self.halo = ORDER - 1
        self.span_x = self.cells_x + self.halo
        self.span_y = self.cells_y + self.halo
        self.window = self.cells_z // nx
        self.octets = self.window // SUBLANES
        self.tiles = -(-self.span_y // nx)
        self.pad_y = self.tiles * nx
        self.rows = self.pad_y * SUBLANES
        self.dests = ny * nx
        self.kept = GRID // 2
        self.width_k = self.kept // self.dests
        self.pad_k = round_up(self.width_k, SUBLANES)
        self.row_k = 2 * self.pad_k
        self.all_y = ny * self.pad_y
        self.pad_x = round_up(self.span_x, SUBLANES)
        self.pack_x = round_up(3 * self.pad_x, LANES)
        self.unroll = 4
        sizes = [len(part) for part in np.array_split(np.arange(self.tiles), 4)]
        self.parts = [(sum(sizes[:i]), size) for i, size in enumerate(sizes)]
        self.most = max(sizes)
        assert nz == 2 and self.cells_z == LANES and self.span_x <= LANES

    def angle(self, outputs, inputs):
        return (outputs[:, None] * inputs[None, :] % GRID) * (2.0 * np.pi / GRID)

    def index_kx(self):
        place = np.arange(self.pad_k)
        index = np.arange(self.dests)[:, None] * self.width_k + np.minimum(place, self.width_k - 1)[None, :]
        return index.reshape(-1), np.tile(place < self.width_k, self.dests)

    def pairs(self, cosine, sine):
        shape = (self.dests, 1, self.pad_k, -1)
        both = np.concatenate([cosine.reshape(shape), sine.reshape(shape)], axis=1)
        return both.reshape(self.dests * self.row_k, -1)

    def x_forward(self):
        local = np.arange(LANES)
        cells = (np.arange(self.nx)[:, None] * self.cells_x + local[None, :]).reshape(-1)
        used = np.tile(local < self.span_x, self.nx)
        index, kept = self.index_kx()
        angle = self.angle(index, cells)
        mask = kept[:, None] * used[None, :]
        return constant_halves(self.pairs(np.cos(angle) * mask, -np.sin(angle) * mask))

    def x_inverse(self):
        lane = np.arange(self.pack_x)
        local = lane % self.pad_x
        cells = (np.arange(self.nx)[:, None] * self.cells_x + local[None, :]).reshape(-1)
        used = np.tile((local < self.span_x) & (lane < 3 * self.pad_x), self.nx)
        index, kept = self.index_kx()
        angle = self.angle(index, cells)
        mask = (kept * np.where(index > 0, 2.0, 1.0))[:, None] * used[None, :]
        return constant_halves(self.pairs(np.cos(angle) * mask, -np.sin(angle) * mask))

    def z_tables(self):
        cells = np.arange(self.cells_z)
        tables = []
        for parity in range(self.nz):
            angle = self.angle(self.nz * cells + parity, cells)
            forward = np.concatenate([np.cos(angle).T, np.sin(angle).T], axis=1)
            inverse = np.concatenate([np.cos(angle), np.sin(angle)], axis=1)
            tables += [constant_halves(forward), constant_halves(inverse)]
        return jnp.stack(tables).reshape(self.nz, 2, 2, self.cells_z, 2 * self.cells_z)

    def y_tables(self):
        local = np.arange(self.pad_y)
        cells = (np.arange(self.ny)[:, None] * self.cells_y + local[None, :]).reshape(-1)
        used = np.tile(local < self.span_y, self.ny)
        angle = self.angle(np.arange(GRID), cells)
        cosine, sine = np.cos(angle) * used[None, :], np.sin(angle) * used[None, :]
        forward = constant_halves(np.concatenate([cosine, sine], axis=1))
        inverse = constant_halves(np.concatenate([cosine.T, sine.T], axis=1))
        return forward, inverse

    def green_lines(self):
        index = np.arange(GRID)
        signed = np.where(2 * index < GRID, index, index - GRID)
        square = (signed * signed).astype(np.float32)
        bspline = 36.0 / (4.0 + 2.0 * np.cos(index * (2.0 * np.pi / GRID))) ** 2
        bspline = np.where(2 * index == GRID, 0.0, bspline).astype(np.float32)
        line_x = np.stack([square, bspline])[:, : self.kept]
        line_y = np.stack([square, bspline])[:, :, None]
        line_z = np.stack([square, bspline]).reshape(2, 1, self.cells_z, self.nz)
        line_z = line_z.transpose(3, 0, 1, 2)
        return jnp.asarray(line_x), jnp.asarray(line_y), jnp.asarray(line_z)


def flipped(value, size, mask):
    result, bit = 0, 1
    while bit < size:
        digit = value // bit % 2
        result = result + bit * ((digit + mask // bit % 2) % 2)
        bit *= 2
    return result


class Group:
    def __init__(self, axes, sizes):
        self.axes, self.sizes = axes, sizes
        self.count = int(np.prod(sizes))
        self.steps = sorted(range(1, self.count), key=lambda mask: -bin(mask).count("1"))

    def index(self, coordinates):
        place = 0
        for axis, size in zip(self.axes, self.sizes):
            place = place * size + coordinates[axis]
        return place

    def me(self):
        return self.index({axis: lax.axis_index(axis) for axis in self.axes})

    def partner(self, mask):
        where = {}
        for axis, size in reversed(list(zip(self.axes, self.sizes))):
            where[axis] = flipped(lax.axis_index(axis), size, mask % size)
            mask //= size
        return where

    def barrier(self):
        semaphore = pltpu.get_barrier_semaphore()
        for step in self.steps:
            pl.semaphore_signal(
                semaphore, inc=1, device_id=self.partner(step), device_id_type=MESH
            )
        pl.semaphore_wait(semaphore, self.count - 1)

    def copies(self, source, target, send_sems, recv_sems):
        result = []
        for step in self.steps:
            where = self.partner(step)
            result.append(
                pltpu.make_async_remote_copy(
                    src_ref=source(self.index(where)),
                    dst_ref=target(self.me()),
                    send_sem=send_sems(step),
                    recv_sem=recv_sems(step),
                    device_id=where,
                    device_id_type=MESH,
                )
            )
        return result


def exchange_kernel(group, same, src_ref, out_ref, send_sems, recv_sems, local_sem):
    me = group.me()
    group.barrier()
    copies = group.copies(
        lambda peer: src_ref if same else src_ref.at[peer],
        lambda place: out_ref.at[place],
        lambda step: send_sems.at[step],
        lambda step: recv_sems.at[step],
    )
    for copy in copies:
        copy.start()
    own = pltpu.make_async_copy(src_ref if same else src_ref.at[me], out_ref.at[me], local_sem)
    own.start()
    own.wait()
    for copy in copies:
        copy.wait()


def group_of(*axes):
    return Group(axes, [lax.axis_size(axis) for axis in axes])


def exchange(data, group, collective_id, same=False):
    shape = ((group.count,) if same else ()) + data.shape
    return pl.pallas_call(
        functools.partial(exchange_kernel, group, same),
        in_specs=[pl.BlockSpec(memory_space=pltpu.VMEM)],
        out_specs=pl.BlockSpec(memory_space=pltpu.VMEM),
        out_shape=jax.ShapeDtypeStruct(shape, data.dtype),
        scratch_shapes=[
            pltpu.SemaphoreType.DMA((group.count,)),
            pltpu.SemaphoreType.DMA((group.count,)),
            pltpu.SemaphoreType.DMA,
        ],
        compiler_params=pltpu.CompilerParams(
            collective_id=collective_id, has_side_effects=True
        ),
    )(data)


def spline_rows(frac):
    rest = 1.0 - frac
    square = frac * frac
    cube = square * frac
    weights = [
        rest * rest * rest / 6.0,
        (3.0 * cube - 6.0 * square + 4.0) / 6.0,
        (-3.0 * cube + 3.0 * square + 3.0 * frac + 1.0) / 6.0,
        cube / 6.0,
    ]
    slopes = [
        -0.5 * rest * rest,
        1.5 * square - 2.0 * frac,
        -1.5 * square + frac + 0.5,
        0.5 * square,
    ]
    return weights, slopes


def placed(offset, values, dim):
    total = jnp.zeros(offset.shape, jnp.float32)
    for k in range(ORDER):
        total = jnp.where(offset == float(k), values[k][dim : dim + 1], total)
    return total


def offsets(rows, lowest):
    return lax.broadcasted_iota(jnp.int32, (rows, LANES), 0).astype(jnp.float32) - lowest


def fold_sign(parity, part):
    return (1 - 2 * lax.rem(parity * part, 2)).astype(jnp.float32)


def list_units(plan, counts_ref, list_ref):
    place = lax.axis_index("gx")

    def block_step(block, total):
        def listed(octet, begin, end, total):
            def put(chunk, total):
                list_ref[total] = (block * plan.chunks + chunk) * plan.octets + octet
                return total + 1

            return lax.fori_loop(begin, end, put, total)

        ends = 0
        for octet in range(plan.octets):
            start = counts_ref[block, place * plan.octets + octet]
            stop = counts_ref[block, LANES // 2 + place * plan.octets + octet]
            begin = start // LANES
            end = jnp.where(stop > start, (stop + LANES - 1) // LANES, begin)
            if octet == 0:
                ends = jnp.where(stop > start, end, 0)
            total = listed(octet, begin, end, total)
        start = counts_ref[block, plan.nx * plan.octets]
        stop = counts_ref[block, LANES // 2 + plan.nx * plan.octets]
        begin = jnp.maximum(start // LANES, ends)
        end = jnp.where((stop > start) & (place == 0), (stop + LANES - 1) // LANES, begin)
        return listed(0, begin, end, total)

    total = lax.fori_loop(0, plan.blocks, block_step, 0)
    for extra in range(plan.unroll):
        list_ref[total + extra] = 0
    return total


def over_units(plan, counts_ref, list_ref, work):
    total = list_units(plan, counts_ref, list_ref)
    parity = lax.axis_index("gz")

    def step(i, carry):
        for lane in range(plan.unroll):
            unit = i * plan.unroll + lane
            code = list_ref[unit]
            octet = lax.rem(code, plan.octets)
            code = lax.div(code, plan.octets)
            chunk, block = lax.rem(code, plan.chunks), lax.div(code, plan.chunks)
            sign = fold_sign(parity, block // plan.nx)
            work(lane, block, chunk, octet, jnp.where(unit < total, sign, 0.0))
        return carry

    lax.fori_loop(0, (total + plan.unroll - 1) // plan.unroll, step, 0)


def z_offsets(plan, octet, lowest):
    first = lax.axis_index("gx") * plan.window + octet * SUBLANES
    offset = offsets(SUBLANES, lowest - first.astype(jnp.float32))
    wraps = offset < float(ORDER - plan.cells_z)
    factor = jnp.where(wraps, fold_sign(lax.axis_index("gz"), 1), 1.0)
    return jnp.where(wraps, offset + float(plan.cells_z), offset), factor


def spread_kernel(plan, counts_ref, atoms_ref, grid_ref, list_ref, y_ref, x_ref, a_ref):
    grid_ref[...] = jnp.zeros_like(grid_ref)
    x_ref[...] = jnp.zeros_like(x_ref)

    def work(lane, block, chunk, octet, sign):
        atoms = atoms_ref[block, :, pl.ds(pl.multiple_of(chunk * LANES, LANES), LANES)]
        weights, _ = spline_rows(atoms[0:3])
        high, low = halves(
            jnp.concatenate(
                [
                    placed(offsets(plan.pad_x, atoms[4:5]), weights, 0),
                    jnp.zeros((LANES - plan.pad_x, LANES), jnp.float32),
                ],
                axis=0,
            )
        )
        x_ref[lane, :LANES, :LANES] = high
        x_ref[lane, :LANES, LANES:] = high
        x_ref[lane, LANES:, :LANES] = low
        y_ref[lane] = placed(offsets(plan.pad_y, atoms[5:6]), weights, 1)
        offset, factor = z_offsets(plan, octet, atoms[6:7])
        line = placed(offset, weights, 2) * factor * (atoms[3:4] * sign)
        for y in range(0, plan.pad_y, 2):
            pair = jnp.concatenate([y_ref[lane, y : y + 1] * line, y_ref[lane, y + 1 : y + 2] * line], axis=0)
            high, low = halves(pair)
            a_ref[lane, y * SUBLANES : (y + 2) * SUBLANES, :LANES] = high
            a_ref[lane, y * SUBLANES : (y + 2) * SUBLANES, LANES:] = low
        product = mm(a_ref[lane], x_ref[lane], ROWS_BY_ROWS)
        place = pl.ds(pl.multiple_of(lax.rem(block, plan.nx) * LANES, LANES), LANES)
        grid_ref[octet, :, place] += product[:, :LANES] + product[:, LANES:]

    over_units(plan, counts_ref, list_ref, work)


def regroup(plan, values):
    shape = values[0].shape
    group = lax.broadcasted_iota(jnp.int32, shape, 1) // plan.window
    moved = []
    for step in range(plan.nx):
        mixed = values[step % plan.nx]
        for part in range(1, plan.nx):
            mixed = jnp.where(group == part, values[(part + step) % plan.nx], mixed)
        moved.append(pltpu.roll(mixed, step * plan.window, 1) if step else mixed)
    results = []
    for part in range(plan.nx):
        result = moved[(-part) % plan.nx]
        for other in range(1, plan.nx):
            result = jnp.where(group == other, moved[(other - part) % plan.nx], result)
        results.append(result)
    return results


def mesh_kernel(
    plan,
    group,
    grid_ref,
    x_forward_ref,
    z_table_ref,
    y_forward_ref,
    y_inverse_ref,
    line_x_ref,
    line_y_ref,
    line_z_ref,
    x_inverse_ref,
    pot_ref,
    there_out_ref,
    there_in_ref,
    back_out_ref,
    back_in_ref,
    u_ref,
    o_ref,
    mid_ref,
    send_sems,
    recv_sems,
    local_sems,
):
    parity = lax.axis_index("gz")
    device = group.me()
    row_k, pad_k, nx = plan.row_k, plan.pad_k, plan.nx
    group.barrier()

    def sending(way, part, out_ref, in_ref):
        first, count = plan.parts[part]
        lanes = pl.ds(first * LANES, count * LANES)
        copies = group.copies(
            lambda peer: out_ref.at[peer, :, lanes],
            lambda place: in_ref.at[place, :, lanes],
            lambda step: send_sems.at[way, part, step],
            lambda step: recv_sems.at[way, part, step],
        )
        own = pltpu.make_async_copy(
            out_ref.at[device, :, lanes], in_ref.at[device, :, lanes], local_sems.at[way, part]
        )
        return copies, own

    def start(copies, own):
        for copy in copies:
            copy.start()
        own.start()

    def arrive(copies, own):
        for copy in copies:
            copy.wait_recv()
        own.wait()

    def tile_lanes(tile):
        return pl.ds(pl.multiple_of(tile * LANES, LANES), LANES)

    def x_forward(tile, carry):
        pieces = []
        for other in range(nx):
            row = pl.multiple_of((tile * nx + other) * SUBLANES, SUBLANES)
            for octet in range(plan.octets):
                pieces.append(grid_ref[octet, pl.ds(row, SUBLANES), :])
        high, low = halves(jnp.concatenate(pieces, axis=0))
        first_pass = mm(x_forward_ref[0], jnp.concatenate([high, low], axis=0), ROWS_BY_ROWS)
        second_pass = mm(x_forward_ref[1], high, ROWS_BY_ROWS)
        total = first_pass[:, :LANES] + (first_pass[:, LANES:] + second_pass)
        there_out_ref[:, :, tile_lanes(tile)] = total.reshape(plan.dests, row_k, LANES)
        return carry

    there = [sending(0, part, there_out_ref, there_in_ref) for part in range(len(plan.parts))]
    back = [sending(1, part, back_out_ref, back_in_ref) for part in range(len(plan.parts))]
    for part, (first, count) in enumerate(plan.parts):
        lax.fori_loop(first, first + count, x_forward, 0)
        start(*there[part])

    def z_transform(direction, rows):
        high = z_table_ref[parity, direction, 0]
        both = jnp.concatenate([high, high], axis=0)
        low = z_table_ref[parity, direction, 1]
        total = mm(u_ref[:rows], both) + mm(u_ref[:rows, :LANES], low)
        return total.reshape(rows // row_k, 2, pad_k, 2 * LANES)

    for part, (first, count) in enumerate(plan.parts):
        arrive(*there[part])
        lines = count * nx

        def z_forward(gy, carry):
            for tile in range(count):
                here = pl.ds((first + tile) * LANES, LANES)
                values = [there_in_ref[gy * nx + gx, :, here] for gx in range(nx)]
                for other, value in enumerate(regroup(plan, values)):
                    row = (tile * nx + other) * row_k
                    high, low = halves(value)
                    u_ref[row : row + row_k, :LANES] = high
                    u_ref[row : row + row_k, LANES:] = low
            total = z_transform(0, lines * row_k)
            real, imag = total[:, 0], total[:, 1]
            row = pl.multiple_of((gy * plan.pad_y + first * nx) * pad_k, pad_k)
            rows = pl.ds(row, lines * pad_k)
            mid_ref[0, rows, :] = (real[..., :LANES] + imag[..., LANES:]).reshape(-1, LANES)
            mid_ref[1, rows, :] = (imag[..., :LANES] - real[..., LANES:]).reshape(-1, LANES)
            return carry

        lax.fori_loop(0, plan.ny, z_forward, 0)

    def column(j):
        lines = pl.ds(j, plan.all_y, stride=pad_k)
        real = mid_ref[0, lines, :]
        imag = mid_ref[1, lines, :]
        stacked = jnp.concatenate(
            [jnp.concatenate([real, imag], axis=1), jnp.concatenate([imag, -real], axis=1)], axis=0
        )
        high, low = halves(stacked)
        spectrum = mm(y_forward_ref[0], high) + (mm(y_forward_ref[0], low) + mm(y_forward_ref[1], high))
        kx = device * plan.width_k + j
        square = (line_y_ref[0] + line_z_ref[parity, 0]) + line_x_ref[0, kx]
        factor = (line_y_ref[1] * line_z_ref[parity, 1]) * line_x_ref[1, kx]
        green = jnp.where(
            square > 0.0,
            coulomb
            * jnp.exp(square * (-np.pi**2 / (ewald * ewald * GRID * GRID)))
            * factor
            / (np.pi * GRID * jnp.maximum(square, 1.0)),
            0.0,
        )
        real = spectrum[:, :LANES] * green
        imag = spectrum[:, LANES:] * green
        stacked = jnp.concatenate(
            [jnp.concatenate([real, imag], axis=1), jnp.concatenate([-imag, real], axis=1)], axis=0
        )
        high, low = halves(stacked)
        result = mm(y_inverse_ref[0], high) + (mm(y_inverse_ref[0], low) + mm(y_inverse_ref[1], high))
        return lines, result

    def columns(i, carry):
        results = [column(i * 2 + other) for other in range(2)]
        for lines, result in results:
            mid_ref[0, lines, :] = result[:, :LANES]
            mid_ref[1, lines, :] = result[:, LANES:]
        return carry

    lax.fori_loop(0, plan.width_k // 2, columns, 0)

    for part, (first, count) in enumerate(plan.parts):
        lines = count * nx

        def z_backward(gy, carry):
            row = pl.multiple_of((gy * plan.pad_y + first * nx) * pad_k, pad_k)
            rows = pl.ds(row, lines * pad_k)
            real = mid_ref[0, rows, :].reshape(lines, pad_k, LANES)
            imag = mid_ref[1, rows, :].reshape(lines, pad_k, LANES)
            high, low = halves(jnp.concatenate([real, imag], axis=1).reshape(-1, LANES))
            u_ref[: lines * row_k, :LANES] = high
            u_ref[: lines * row_k, LANES:] = low
            total = z_transform(1, lines * row_k)
            real, imag = total[:, 0], total[:, 1]
            result = jnp.concatenate(
                [real[..., :LANES] - imag[..., LANES:], imag[..., :LANES] + real[..., LANES:]], axis=1
            )
            o_ref[: lines * row_k] = result.reshape(-1, LANES)
            for tile in range(count):
                values = []
                for other in range(nx):
                    row = (tile * nx + other) * row_k
                    values.append(o_ref[row : row + row_k])
                here = pl.ds((first + tile) * LANES, LANES)
                for gx, value in enumerate(regroup(plan, values)):
                    back_out_ref[gy * nx + gx, :, here] = value
            return carry

        lax.fori_loop(0, plan.ny, z_backward, 0)
        start(*back[part])

    def x_inverse(tile, carry):
        lines = back_in_ref[:, :, tile_lanes(tile)].reshape(plan.dests * row_k, LANES)
        high, low = halves(lines.T)
        first_pass = mm(jnp.concatenate([high, low], axis=0), x_inverse_ref[0])
        value = first_pass[:LANES] + (first_pass[LANES:] + mm(high, x_inverse_ref[1]))
        lane = lax.rem(lax.broadcasted_iota(jnp.int32, value.shape, 1), plan.pack_x)
        rest = value - value.astype(jnp.bfloat16).astype(jnp.float32)
        value = jnp.where((lane >= plan.pad_x) & (lane < 2 * plan.pad_x), rest, value)
        for octet in range(plan.octets):
            for other in range(0, nx, 2):
                pieces = []
                for extra in range(2):
                    row = (other + extra) * plan.window + octet * SUBLANES
                    pieces.append(value[row : row + SUBLANES])
                row = pl.multiple_of((tile * nx + other) * SUBLANES, 2 * SUBLANES)
                pot_ref[octet, pl.ds(row, 2 * SUBLANES), :] = jnp.concatenate(pieces, axis=0).astype(jnp.bfloat16)
        return carry

    for part, (first, count) in enumerate(plan.parts):
        arrive(*back[part])
        lax.fori_loop(first, first + count, x_inverse, 0)
    for copies, _ in there + back:
        for copy in copies:
            copy.wait_send()


def gather_kernel(plan, counts_ref, atoms_ref, pot_ref, out_ref, list_ref, y_ref, x_ref, p_ref):
    out_ref[...] = jnp.zeros_like(out_ref)
    pack = plan.pack_x

    def work(lane, block, chunk, octet, sign):
        atoms = atoms_ref[block, :, pl.ds(pl.multiple_of(chunk * LANES, LANES), LANES)]
        weights, slopes = spline_rows(atoms[0:3])
        offset = offsets(plan.pad_x, atoms[4:5])
        table = jnp.concatenate([placed(offset, weights, 0), placed(offset, slopes, 0)], axis=1)
        high = table.astype(jnp.bfloat16).astype(jnp.float32)
        unused = jnp.zeros((pack - 3 * plan.pad_x, 2 * LANES), jnp.float32)
        x_ref[lane] = jnp.concatenate([high, high, table - high, unused], axis=0).astype(jnp.bfloat16)
        offset = offsets(plan.pad_y, atoms[5:6])
        y_ref[lane, 0] = placed(offset, weights, 1)
        y_ref[lane, 1] = placed(offset, slopes, 1)
        offset, factor = z_offsets(plan, octet, atoms[6:7])
        factor = factor * sign
        weight_z = placed(offset, weights, 2) * factor
        slope_z = placed(offset, slopes, 2) * factor
        place = pl.ds(pl.multiple_of(lax.rem(block, plan.nx) * pack, LANES), pack)
        p_ref[lane] = mm(pot_ref[octet, :, place], x_ref[lane])
        total_x = jnp.zeros((SUBLANES, LANES), jnp.float32)
        total_y = jnp.zeros((SUBLANES, LANES), jnp.float32)
        total_z = jnp.zeros((SUBLANES, LANES), jnp.float32)
        for y in range(plan.pad_y):
            rows = slice(y * SUBLANES, (y + 1) * SUBLANES)
            plain = p_ref[lane, rows, :LANES]
            weight = y_ref[lane, 0, y : y + 1]
            total_x += weight * p_ref[lane, rows, LANES:]
            total_y += y_ref[lane, 1, y : y + 1] * plain
            total_z += weight * plain
        totals = [weight_z * total_x, weight_z * total_y, slope_z * total_z]
        for dim in range(3):
            row = jnp.sum(totals[dim], axis=0, keepdims=True)
            out_ref[block, pl.ds(dim * plan.chunks + chunk, 1), :] += row

    over_units(plan, counts_ref, list_ref, work)


def vmem_call(kernel, out_shape, scratch_shapes, smem=(), **params):
    def call(*operands):
        specs = [
            pl.BlockSpec(memory_space=pltpu.SMEM if i in smem else pltpu.VMEM)
            for i in range(len(operands))
        ]
        return pl.pallas_call(
            kernel,
            in_specs=specs,
            out_specs=pl.BlockSpec(memory_space=pltpu.VMEM),
            out_shape=out_shape,
            scratch_shapes=scratch_shapes,
            compiler_params=pltpu.CompilerParams(vmem_limit_bytes=50 * 2**20, **params),
        )(*operands)

    return call


def per_device(charges, fractions, base_cells, counts):
    capacity = charges.shape[0]
    plan = Plan(lax.axis_size("gz"), lax.axis_size("gy"), lax.axis_size("gx"), capacity)
    f32, bf16 = jnp.float32, jnp.bfloat16
    slot = jnp.arange(capacity, dtype=jnp.int32)
    live = slot < counts.reshape(())
    charge = jnp.where(live, charges, jnp.zeros_like(charges))
    local_x = (base_cells[0] - lax.axis_index("gx") * plan.cells_x).astype(f32)
    local_y = (base_cells[1] - lax.axis_index("gy") * plan.cells_y).astype(f32)
    key = jnp.where(live, base_cells[2] - lax.axis_index("gz") * plan.cells_z, plan.cells_z)
    key, slot, t_x, t_y, t_z, charge, local_x, local_y = lax.sort(
        [key, slot, fractions[0], fractions[1], fractions[2], charge, local_x, local_y],
        num_keys=1,
        is_stable=False,
    )
    edges = np.full(LANES, -1)
    starts = np.arange(plan.nx * plan.octets + 1) * SUBLANES
    edges[: len(starts)] = starts - plan.halo
    edges[LANES // 2 : LANES // 2 + len(starts)] = np.minimum(starts + SUBLANES, plan.cells_z)
    counted = jnp.sum((key[None, :] < jnp.asarray(edges)[:, None]).astype(f32), axis=1)
    counted = jnp.pad(counted, (0, capacity - LANES))
    atoms = jnp.stack([t_x, t_y, t_z, charge, local_x, local_y, key.astype(f32), counted])
    atoms = exchange(atoms, group_of("gz", "gx"), 0, same=True)
    counts = atoms[:, 7, :LANES].astype(jnp.int32)

    lanes = plan.tiles * LANES
    mesh_shape = (plan.octets, plan.rows, plan.nx * LANES)
    units = plan.blocks * plan.chunks * plan.octets + plan.unroll
    grid = vmem_call(
        functools.partial(spread_kernel, plan),
        jax.ShapeDtypeStruct(mesh_shape, f32),
        [
            pltpu.SMEM((units,), jnp.int32),
            pltpu.VMEM((plan.unroll, plan.pad_y, LANES), f32),
            pltpu.VMEM((plan.unroll, 2 * LANES, 2 * LANES), bf16),
            pltpu.VMEM((plan.unroll, plan.rows, 2 * LANES), bf16),
        ],
        smem=(0,),
    )(counts, atoms)
    y_forward, y_inverse = plan.y_tables()
    line_x, line_y, line_z = plan.green_lines()
    group = group_of("gy", "gx")
    parts = len(plan.parts)
    half = pltpu.VMEM((plan.dests, plan.row_k, lanes), f32)
    potential = vmem_call(
        functools.partial(mesh_kernel, plan, group),
        jax.ShapeDtypeStruct((plan.octets, plan.rows, plan.nx * plan.pack_x), bf16),
        [
            half,
            half,
            half,
            half,
            pltpu.VMEM((plan.most * plan.nx * plan.row_k, 2 * LANES), bf16),
            pltpu.VMEM((plan.most * plan.nx * plan.row_k, LANES), f32),
            pltpu.VMEM((2, plan.all_y * plan.pad_k, LANES), f32),
            pltpu.SemaphoreType.DMA((2, parts, group.count)),
            pltpu.SemaphoreType.DMA((2, parts, group.count)),
            pltpu.SemaphoreType.DMA((2, parts)),
        ],
        smem=(5,),
        collective_id=1,
        has_side_effects=True,
    )(
        grid,
        plan.x_forward(),
        plan.z_tables(),
        y_forward,
        y_inverse,
        line_x,
        line_y,
        line_z,
        plan.x_inverse(),
    )
    shares = vmem_call(
        functools.partial(gather_kernel, plan),
        jax.ShapeDtypeStruct((plan.blocks, 3 * plan.chunks, LANES), f32),
        [
            pltpu.SMEM((units,), jnp.int32),
            pltpu.VMEM((plan.unroll, 2, plan.pad_y, LANES), f32),
            pltpu.VMEM((plan.unroll, plan.pack_x, 2 * LANES), bf16),
            pltpu.VMEM((plan.unroll, plan.rows, 2 * LANES), f32),
        ],
        smem=(0,),
    )(counts, atoms, potential)
    shares = exchange(shares, group_of("gz", "gx"), 2)
    forces = -charge[None, :] * jnp.sum(shares, axis=0).reshape(3, capacity)
    result = lax.sort([slot, forces[0], forces[1], forces[2]], num_keys=1, is_stable=False)
    return jnp.stack(result[1:])


def solution(mesh):
    in_specs = (
        P(("gz", "gy", "gx")),
        P(None, ("gz", "gy", "gx")),
        P(None, ("gz", "gy", "gx")),
        P("gz", "gy", "gx"),
    )
    out_specs = P(None, ("gz", "gy", "gx"))
    return jax.shard_map(
        per_device, mesh=mesh, in_specs=in_specs, out_specs=out_specs, check_vma=False
    )
```

time: 216 us -> 155 us (0.72)
  Pallas kernels: 189 us -> 135 us
  local copies, waits for them, and re-layouts: 10.4 us -> 4.16 us
    pallas_call x4 -> x2, Pallas kernels: 99.9 us -> 31.5 us  [exchange(): pl.pallas_call(functools.partial(exchange_kernel, group, same), in_specs=...]
    pallas_call x3, Pallas kernels: 89.6 us -> 104 us  [call(): pl.pallas_call(kernel, in_specs=specs, out_specs=pl.BlockSpec(memory_spac...]
    unnamed x26 -> x22, local copies, waits for them, and re-layouts: 5.75 us -> 1.74 us
where the time goes in v2:
time: 155 us; the launch traced here: 153 us
  Pallas kernels  135 us (87%)
  other arithmetic  13.3 us (9%)
  local copies, waits for them, and re-layouts  4.16 us (3%)
    pallas_call x3, Pallas kernels, call(): pl.pallas_call(kernel, in_specs=specs, out_specs=pl.BlockSpec(memory_spac...  104 us
    pallas_call x2, Pallas kernels, exchange(): pl.pallas_call(functools.partial(exchange_kernel, group, same), in_specs=...  31.5 us
    sort x1, other arithmetic, per_device(): lax.sort([slot, forces[0], forces[1], forces[2]], num_keys=1, is_stable=F...  4.89 us
    sort x1, other arithmetic, per_device(): lax.sort([key, slot, fractions[0], fractions[1], fractions[2], charge, lo...  4.33 us

profile of v2, /device:TPU:0, one launch (start us, length us, event | category | flops | bytes accessed | tf_op | source)
XLA Modules:
  0.0 153.4 jit_solution(16812609185881800184)
XLA Ops:
  0.7 0.7 fusion
  1.5 0.9 subtract_convert_fusion
  2.4 0.9 fusion.3
  3.3 4.3 %sort.78 = (s32[2048]{0:T(1024)S(1)}, s32[2048]{0:T(1024)S(1)}, f32[2048]{0:T(1024)S(1)}, f32[2048]{0:T(1024)S(1)}, f32[2048]{0:T(1024)S(1)}, /*index=5*/f32[2048]{0:T(1024)S(1)}, f32[2048]{0:T(1024)S(1)}, f32[2048]{0:T(1024)S(1)}) sort(s32[2048]{0:T(1024)S(1)} %fusion.1, s32[2048]{0:T(1024)S(1)} %iota.6, f32[2048]{0:T(1024)S(1)} %bitcast.36, ...), dimensions={0}, to_apply=%region_0.1 | sort | flops 22528 | bytes 131072 | tf_op jit(solution)/shard_map/sort | solution.py:645
  7.6 0.9 convert_reduce_fusion
  8.5 0.7 stack.59.src_ref
  9.2 20.0 %shard_map.154.atoms_ref = f32[8,8,2048]{2,1,0:T(8,128)} custom-call(f32[8,2048]{1,0:T(8,128)} %stack.59.src_ref), custom_call_target="tpu_custom_call" | custom-call | tf_op jit(solution)/shard_map/pallas_call | solution.py:219
  29.3 0.8 slice.36
  30.0 1.0 copy-done
  31.1 0.0 copy-start.8
  31.1 14.2 %shard_map.155.grid_ref = f32[4,544,512]{2,1,0:T(8,128)} custom-call(s32[8,128]{1,0:T(8,128)S(1)} %convert_bitcast_fusion.counts_ref, f32[8,8,2048]{2,1,0:T(8,128)S(1)} %copy-done), custom_call_target="tpu_custom_call" | custom-call | tf_op jit(solution)/shard_map/pallas_call | solution.py:623
  45.3 0.0 copy-done.2
  45.3 0.0 copy-done.9
  45.3 0.0 copy-done.10
  45.3 0.0 copy-done.4
  45.3 0.0 copy-done.5
  45.3 0.0 copy-done.6
  45.4 76.6 %shard_map.156.pot_ref = bf16[4,544,1024]{2,1,0:T(8,128)(2,1)} custom-call(f32[4,544,512]{2,1,0:T(8,128)} %shard_map.155.grid_ref, bf16[2,256,512]{2,1,0:T(8,128)(2,1)S(1)} %copy-done.7, bf16[2,2,2,128,256]{4,3,2,1,0:T(8,128)(2,1)S(1)} %copy-done.6, bf16[2,256,544]{2,1,0:T(8,128)(2,1)S(1)} %copy-done.4, bf16[2,272,512]{2,1,0:T(8,128)(2,1)S(1)} %copy-done.5, ...), custom_call_target="tpu_custom_call" | custom-call | tf_op jit(solution)/shard_map/pallas_call | solution.py:623
  122.0 12.7 %shard_map.157.src_ref = f32[8,48,128]{2,1,0:T(8,128)S(1)} custom-call(s32[8,128]{1,0:T(8,128)S(1)} %convert_bitcast_fusion.counts_ref, f32[8,8,2048]{2,1,0:T(8,128)S(1)} %copy-done.1, bf16[4,544,1024]{2,1,0:T(8,128)(2,1)} %shard_map.156.pot_ref), custom_call_target="tpu_custom_call" | custom-call | tf_op jit(solution)/shard_map/pallas_call | solution.py:623
  134.7 0.7 copy-done.3
  135.4 11.5 %shard_map.158 = f32[8,48,128]{2,1,0:T(8,128)} custom-call(f32[8,48,128]{2,1,0:T(8,128)} %copy-done.3), custom_call_target="tpu_custom_call" | custom-call | tf_op jit(solution)/shard_map/pallas_call | solution.py:219
  146.9 0.9 reduce_sum.19
  147.9 4.9 %sort.79 = (s32[2048]{0:T(1024)}, f32[2048]{0:T(1024)S(1)}, f32[2048]{0:T(1024)S(1)}, f32[2048]{0:T(1024)S(1)}) sort(s32[2048]{0:T(1024)S(1)} %get-tuple-element.16, f32[2048]{0:T(1024)S(1)} %bitcast.34, f32[2048]{0:T(1024)S(1)} %bitcast.33, f32[2048]{0:T(1024)S(1)} %bitcast.32), dimensions={0}, to_apply=%region_3.4 | sort | flops 22528 | bytes 65536 | tf_op jit(solution)/shard_map/sort | solution.py:721
  152.8 0.6 pad_maximum_fusion
  (22 shorter events, 0.1 us)
Async XLA Ops:
  0.0 45.3 %copy-start.2 = (bf16[2,256,1024]{2,1,0:T(8,128)(2,1)S(1)}, bf16[2,256,1024]{2,1,0:T(8,128)(2,1)}, u32[]{:S(2)}) copy-start(bf16[2,256,1024]{2,1,0:T(8,128)(2,1)} %constant.54.clone.x_inverse_ref) | copy-start | bytes 3145732
  0.0 45.3 %copy-start.9 = (f32[2,2,1,128]{3,2,1,0:T(1,128)S(1)}, f32[2,2,1,128]{3,2,1,0:T(1,128)}, u32[]{:S(2)}) copy-start(f32[2,2,1,128]{3,2,1,0:T(1,128)} %constant.49.clone.line_z_ref) | copy-start | bytes 6148
  0.0 45.3 %copy-start.10 = (f32[2,128]{1,0:T(2,128)S(1)}, f32[2,128]{1,0:T(2,128)}, u32[]{:S(2)}) copy-start(f32[2,128]{1,0:T(2,128)} %constant.47.clone.line_x_ref) | copy-start | bytes 3076
  30.0 1.0 copy-start
  31.1 14.3 %copy-start.4 = (bf16[2,256,544]{2,1,0:T(8,128)(2,1)S(1)}, bf16[2,256,544]{2,1,0:T(8,128)(2,1)}, u32[]{:S(2)}) copy-start(bf16[2,256,544]{2,1,0:T(8,128)(2,1)} %constant.45.clone.y_forward_ref) | copy-start | bytes 1671172
  31.1 14.3 %copy-start.5 = (bf16[2,272,512]{2,1,0:T(8,128)(2,1)S(1)}, bf16[2,272,512]{2,1,0:T(8,128)(2,1)}, u32[]{:S(2)}) copy-start(bf16[2,272,512]{2,1,0:T(8,128)(2,1)} %constant.46.clone.y_inverse_ref) | copy-start | bytes 1671172
  31.1 14.3 %copy-start.6 = (bf16[2,2,2,128,256]{4,3,2,1,0:T(8,128)(2,1)S(1)}, bf16[2,2,2,128,256]{4,3,2,1,0:T(8,128)(2,1)}, u32[]{:S(2)}) copy-start(bf16[2,2,2,128,256]{4,3,2,1,0:T(8,128)(2,1)} %constant.62.z_table_ref) | copy-start | bytes 1572868
  31.1 14.3 %copy-start.7 = (bf16[2,256,512]{2,1,0:T(8,128)(2,1)S(1)}, bf16[2,256,512]{2,1,0:T(8,128)(2,1)}, u32[]{:S(2)}) copy-start(bf16[2,256,512]{2,1,0:T(8,128)(2,1)} %constant.50.clone.x_forward_ref) | copy-start | bytes 1572868
  31.1 14.3 %copy-start.8 = (f32[2,256,1]{2,1,0:T(8,128)S(1)}, f32[2,256,1]{2,1,0:T(8,128)}, u32[]{:S(2)}) copy-start(f32[2,256,1]{2,1,0:T(8,128)} %constant.48.clone.line_y_ref) | copy-start | bytes 6148
  45.4 76.6 %copy-start.1 = (f32[8,8,2048]{2,1,0:T(8,128)S(1)}, f32[8,8,2048]{2,1,0:T(8,128)}, u32[]{:S(2)}) copy-start(f32[8,8,2048]{2,1,0:T(8,128)} %shard_map.154.atoms_ref) | copy-start | bytes 1572868
  134.7 0.7 copy-start.3

commit v3 on v2

--- a/solution.py
+++ b/solution.py
@@ -60,28 +60,28 @@
         self.dests = ny * nx
         self.kept = GRID // 2
         self.width_k = self.kept // self.dests
-        self.pad_k = round_up(self.width_k, SUBLANES)
-        self.row_k = 2 * self.pad_k
+        self.half_k = SUBLANES // 2
+        self.groups = -(-self.width_k // self.half_k)
+        self.row_k = self.groups * SUBLANES
         self.all_y = ny * self.pad_y
         self.pad_x = round_up(self.span_x, SUBLANES)
         self.pack_x = round_up(3 * self.pad_x, LANES)
         self.unroll = 4
         sizes = [len(part) for part in np.array_split(np.arange(self.tiles), 4)]
         self.parts = [(sum(sizes[:i]), size) for i, size in enumerate(sizes)]
-        self.most = max(sizes)
         assert nz == 2 and self.cells_z == LANES and self.span_x <= LANES
 
     def angle(self, outputs, inputs):
         return (outputs[:, None] * inputs[None, :] % GRID) * (2.0 * np.pi / GRID)
 
     def index_kx(self):
-        place = np.arange(self.pad_k)
+        place = np.arange(self.groups * self.half_k)
         index = np.arange(self.dests)[:, None] * self.width_k + np.minimum(place, self.width_k - 1)[None, :]
         return index.reshape(-1), np.tile(place < self.width_k, self.dests)
 
     def pairs(self, cosine, sine):
-        shape = (self.dests, 1, self.pad_k, -1)
-        both = np.concatenate([cosine.reshape(shape), sine.reshape(shape)], axis=1)
+        shape = (self.dests, self.groups, self.half_k, -1)
+        both = np.concatenate([cosine.reshape(shape), sine.reshape(shape)], axis=2)
         return both.reshape(self.dests * self.row_k, -1)
 
     def x_forward(self):
@@ -166,14 +166,6 @@
             where[axis] = flipped(lax.axis_index(axis), size, mask % size)
             mask //= size
         return where
-
-    def barrier(self):
-        semaphore = pltpu.get_barrier_semaphore()
-        for step in self.steps:
-            pl.semaphore_signal(
-                semaphore, inc=1, device_id=self.partner(step), device_id_type=MESH
-            )
-        pl.semaphore_wait(semaphore, self.count - 1)
 
     def copies(self, source, target, send_sems, recv_sems):
         result = []
@@ -192,44 +184,82 @@
         return result
 
 
-def exchange_kernel(group, same, src_ref, out_ref, send_sems, recv_sems, local_sem):
-    me = group.me()
-    group.barrier()
-    copies = group.copies(
-        lambda peer: src_ref if same else src_ref.at[peer],
-        lambda place: out_ref.at[place],
-        lambda step: send_sems.at[step],
-        lambda step: recv_sems.at[step],
+def greet(groups):
+    semaphore = pltpu.get_barrier_semaphore()
+    for group in groups:
+        for step in group.steps:
+            pl.semaphore_signal(
+                semaphore, inc=1, device_id=group.partner(step), device_id_type=MESH
+            )
+    pl.semaphore_wait(semaphore, sum(group.count - 1 for group in groups))
+
+
+def atoms_kernel(across, along, src_ref, out_ref, send_sems, recv_sems, local_sem):
+    mine = across.me() * along.count + along.me()
+    greet([across, along])
+
+    def sends(group, source, place, row):
+        return group.copies(
+            lambda peer: source,
+            lambda me: out_ref.at[place],
+            lambda step: send_sems.at[row, step],
+            lambda step: recv_sems.at[row, step],
+        )
+
+    crossing = sends(across, src_ref, mine, 0)
+    direct = sends(along, src_ref, mine, 1)
+    for copy in crossing + direct:
+        copy.start()
+    own = pltpu.make_async_copy(src_ref, out_ref.at[mine], local_sem)
+    own.start()
+    forwarded = []
+    for row, (step, copy) in enumerate(zip(across.steps, crossing)):
+        copy.wait_recv()
+        theirs = across.index(across.partner(step)) * along.count + along.me()
+        forwarded += sends(along, out_ref.at[theirs], theirs, 2 + row)
+    for copy in forwarded:
+        copy.start()
+    own.wait()
+    for copy in crossing:
+        copy.wait_send()
+    for copy in direct + forwarded:
+        copy.wait()
+
+
+def shares_kernel(across, along, src_ref, out_ref, sum_ref, first_ref, second_ref, send_sems, recv_sems):
+    greet([across, along])
+    first = along.copies(
+        lambda peer: src_ref.at[peer],
+        lambda me: first_ref.at[me],
+        lambda step: send_sems.at[0, step],
+        lambda step: recv_sems.at[0, step],
     )
-    for copy in copies:
+    for copy in first:
         copy.start()
-    own = pltpu.make_async_copy(src_ref if same else src_ref.at[me], out_ref.at[me], local_sem)
-    own.start()
-    own.wait()
-    for copy in copies:
-        copy.wait()
+    total = src_ref[along.me()]
+    for step, copy in zip(along.steps, first):
+        copy.wait_recv()
+        total = total + first_ref[along.index(along.partner(step))]
+    sum_ref[...] = total
+    second = across.copies(
+        lambda peer: sum_ref.at[peer],
+        lambda me: second_ref.at[me],
+        lambda step: send_sems.at[1, step],
+        lambda step: recv_sems.at[1, step],
+    )
+    for copy in second:
+        copy.start()
+    result = sum_ref[across.me()]
+    for step, copy in zip(across.steps, second):
+        copy.wait_recv()
+        result = result + second_ref[across.index(across.partner(step))]
+    out_ref[...] = result
+    for copy in first + second:
+        copy.wait_send()
 
 
 def group_of(*axes):
     return Group(axes, [lax.axis_size(axis) for axis in axes])
-
-
-def exchange(data, group, collective_id, same=False):
-    shape = ((group.count,) if same else ()) + data.shape
-    return pl.pallas_call(
-        functools.partial(exchange_kernel, group, same),
-        in_specs=[pl.BlockSpec(memory_space=pltpu.VMEM)],
-        out_specs=pl.BlockSpec(memory_space=pltpu.VMEM),
-        out_shape=jax.ShapeDtypeStruct(shape, data.dtype),
-        scratch_shapes=[
-            pltpu.SemaphoreType.DMA((group.count,)),
-            pltpu.SemaphoreType.DMA((group.count,)),
-            pltpu.SemaphoreType.DMA,
-        ],
-        compiler_params=pltpu.CompilerParams(
-            collective_id=collective_id, has_side_effects=True
-        ),
-    )(data)
 
 
 def spline_rows(frac):
@@ -402,20 +432,24 @@
 ):
     parity = lax.axis_index("gz")
     device = group.me()
-    row_k, pad_k, nx = plan.row_k, plan.pad_k, plan.nx
-    group.barrier()
-
-    def sending(way, part, out_ref, in_ref):
-        first, count = plan.parts[part]
+    row_k, nx = plan.row_k, plan.nx
+    greet([group])
+
+    def sending(way, kind, part, out_ref, in_ref):
+        first, count = part
         lanes = pl.ds(first * LANES, count * LANES)
+        rows = pl.ds(kind * SUBLANES, SUBLANES)
+        slot = plan.parts.index(part) if part in plan.parts else 0
         copies = group.copies(
-            lambda peer: out_ref.at[peer, :, lanes],
-            lambda place: in_ref.at[place, :, lanes],
-            lambda step: send_sems.at[way, part, step],
-            lambda step: recv_sems.at[way, part, step],
+            lambda peer: out_ref.at[peer, rows, lanes],
+            lambda place: in_ref.at[place, rows, lanes],
+            lambda step: send_sems.at[way, kind, slot, step],
+            lambda step: recv_sems.at[way, kind, slot, step],
         )
         own = pltpu.make_async_copy(
-            out_ref.at[device, :, lanes], in_ref.at[device, :, lanes], local_sems.at[way, part]
+            out_ref.at[device, rows, lanes],
+            in_ref.at[device, rows, lanes],
+            local_sems.at[way, kind, slot],
         )
         return copies, own
 
@@ -445,52 +479,54 @@
         there_out_ref[:, :, tile_lanes(tile)] = total.reshape(plan.dests, row_k, LANES)
         return carry
 
-    there = [sending(0, part, there_out_ref, there_in_ref) for part in range(len(plan.parts))]
-    back = [sending(1, part, back_out_ref, back_in_ref) for part in range(len(plan.parts))]
+    whole = [(0, plan.tiles)]
+    kinds = range(plan.groups)
+    there = [
+        [sending(0, kind, part, there_out_ref, there_in_ref) for part in (whole if kind else plan.parts)]
+        for kind in kinds
+    ]
+    back = [[sending(1, kind, part, back_out_ref, back_in_ref) for part in plan.parts] for kind in kinds]
     for part, (first, count) in enumerate(plan.parts):
         lax.fori_loop(first, first + count, x_forward, 0)
-        start(*there[part])
+        start(*there[0][part])
+    for kind in kinds[1:]:
+        start(*there[kind][0])
+
+    imaginary = lax.broadcasted_iota(jnp.int32, (1, SUBLANES, 1), 1) >= plan.half_k
 
     def z_transform(direction, rows):
         high = z_table_ref[parity, direction, 0]
         both = jnp.concatenate([high, high], axis=0)
         low = z_table_ref[parity, direction, 1]
         total = mm(u_ref[:rows], both) + mm(u_ref[:rows, :LANES], low)
-        return total.reshape(rows // row_k, 2, pad_k, 2 * LANES)
-
-    for part, (first, count) in enumerate(plan.parts):
-        arrive(*there[part])
-        lines = count * nx
-
-        def z_forward(gy, carry):
-            for tile in range(count):
-                here = pl.ds((first + tile) * LANES, LANES)
-                values = [there_in_ref[gy * nx + gx, :, here] for gx in range(nx)]
-                for other, value in enumerate(regroup(plan, values)):
-                    row = (tile * nx + other) * row_k
-                    high, low = halves(value)
-                    u_ref[row : row + row_k, :LANES] = high
-                    u_ref[row : row + row_k, LANES:] = low
-            total = z_transform(0, lines * row_k)
-            real, imag = total[:, 0], total[:, 1]
-            row = pl.multiple_of((gy * plan.pad_y + first * nx) * pad_k, pad_k)
-            rows = pl.ds(row, lines * pad_k)
-            mid_ref[0, rows, :] = (real[..., :LANES] + imag[..., LANES:]).reshape(-1, LANES)
-            mid_ref[1, rows, :] = (imag[..., :LANES] - real[..., LANES:]).reshape(-1, LANES)
-            return carry
-
-        lax.fori_loop(0, plan.ny, z_forward, 0)
-
-    def column(j):
-        lines = pl.ds(j, plan.all_y, stride=pad_k)
-        real = mid_ref[0, lines, :]
-        imag = mid_ref[1, lines, :]
+        total = total.reshape(rows // SUBLANES, SUBLANES, 2 * LANES)
+        swapped = pltpu.roll(total[..., LANES:], plan.half_k, 1)
+        swapped = jnp.where(imaginary == (direction == 0), -swapped, swapped)
+        return (total[..., :LANES] + swapped).reshape(rows, LANES)
+
+    def z_forward(kind, gy):
+        rows = slice(kind * SUBLANES, (kind + 1) * SUBLANES)
+        for tile in range(plan.tiles):
+            here = pl.ds(tile * LANES, LANES)
+            values = regroup(plan, [there_in_ref[gy * nx + gx, rows, here] for gx in range(nx)])
+            for other in range(0, nx, 2):
+                row = (tile * nx + other) * SUBLANES
+                high, low = halves(jnp.concatenate(values[other : other + 2], axis=0))
+                u_ref[row : row + 2 * SUBLANES, :LANES] = high
+                u_ref[row : row + 2 * SUBLANES, LANES:] = low
+        row = pl.multiple_of(gy * plan.rows, SUBLANES)
+        mid_ref[kind, pl.ds(row, plan.rows), :] = z_transform(0, plan.rows)
+
+    def column(kind, j):
+        lines = [pl.ds(j + half * plan.half_k, plan.all_y, stride=SUBLANES) for half in range(2)]
+        real = mid_ref[kind, lines[0], :]
+        imag = mid_ref[kind, lines[1], :]
         stacked = jnp.concatenate(
             [jnp.concatenate([real, imag], axis=1), jnp.concatenate([imag, -real], axis=1)], axis=0
         )
         high, low = halves(stacked)
         spectrum = mm(y_forward_ref[0], high) + (mm(y_forward_ref[0], low) + mm(y_forward_ref[1], high))
-        kx = device * plan.width_k + j
+        kx = device * plan.width_k + kind * plan.half_k + j
         square = (line_y_ref[0] + line_z_ref[parity, 0]) + line_x_ref[0, kx]
         factor = (line_y_ref[1] * line_z_ref[parity, 1]) * line_x_ref[1, kx]
         green = jnp.where(
@@ -510,44 +546,45 @@
         result = mm(y_inverse_ref[0], high) + (mm(y_inverse_ref[0], low) + mm(y_inverse_ref[1], high))
         return lines, result
 
-    def columns(i, carry):
-        results = [column(i * 2 + other) for other in range(2)]
+    def columns(kind, i):
+        results = [column(kind, i * 2 + other) for other in range(2)]
         for lines, result in results:
-            mid_ref[0, lines, :] = result[:, :LANES]
-            mid_ref[1, lines, :] = result[:, LANES:]
-        return carry
-
-    lax.fori_loop(0, plan.width_k // 2, columns, 0)
-
-    for part, (first, count) in enumerate(plan.parts):
-        lines = count * nx
-
-        def z_backward(gy, carry):
-            row = pl.multiple_of((gy * plan.pad_y + first * nx) * pad_k, pad_k)
-            rows = pl.ds(row, lines * pad_k)
-            real = mid_ref[0, rows, :].reshape(lines, pad_k, LANES)
-            imag = mid_ref[1, rows, :].reshape(lines, pad_k, LANES)
-            high, low = halves(jnp.concatenate([real, imag], axis=1).reshape(-1, LANES))
-            u_ref[: lines * row_k, :LANES] = high
-            u_ref[: lines * row_k, LANES:] = low
-            total = z_transform(1, lines * row_k)
-            real, imag = total[:, 0], total[:, 1]
-            result = jnp.concatenate(
-                [real[..., :LANES] - imag[..., LANES:], imag[..., :LANES] + real[..., LANES:]], axis=1
-            )
-            o_ref[: lines * row_k] = result.reshape(-1, LANES)
-            for tile in range(count):
-                values = []
-                for other in range(nx):
-                    row = (tile * nx + other) * row_k
-                    values.append(o_ref[row : row + row_k])
-                here = pl.ds((first + tile) * LANES, LANES)
-                for gx, value in enumerate(regroup(plan, values)):
-                    back_out_ref[gy * nx + gx, :, here] = value
+            mid_ref[kind, lines[0], :] = result[:, :LANES]
+            mid_ref[kind, lines[1], :] = result[:, LANES:]
+
+    def z_backward(kind, part, gy):
+        first, count = part
+        size = count * nx * SUBLANES
+        row = pl.multiple_of(gy * plan.rows + first * nx * SUBLANES, SUBLANES)
+        high, low = halves(mid_ref[kind, pl.ds(row, size), :])
+        u_ref[:size, :LANES] = high
+        u_ref[:size, LANES:] = low
+        o_ref[:size] = z_transform(1, size)
+        for tile in range(count):
+            values = []
+            for other in range(nx):
+                row = (tile * nx + other) * SUBLANES
+                values.append(o_ref[row : row + SUBLANES])
+            here = pl.ds((first + tile) * LANES, LANES)
+            rows = slice(kind * SUBLANES, (kind + 1) * SUBLANES)
+            for gx, value in enumerate(regroup(plan, values)):
+                back_out_ref[gy * nx + gx, rows, here] = value
+
+    def each(count, work, *fixed):
+        def step(i, carry):
+            work(*fixed, i)
             return carry
 
-        lax.fori_loop(0, plan.ny, z_backward, 0)
-        start(*back[part])
+        lax.fori_loop(0, count, step, 0)
+
+    for kind in kinds:
+        for piece in there[kind]:
+            arrive(*piece)
+        each(plan.ny, z_forward, kind)
+        each(min(plan.half_k, plan.width_k) // 2, columns, kind)
+        for part, piece in zip(plan.parts, back[kind]):
+            each(plan.ny, z_backward, kind, part)
+            start(*piece)
 
     def x_inverse(tile, carry):
         lines = back_in_ref[:, :, tile_lanes(tile)].reshape(plan.dests * row_k, LANES)
@@ -568,11 +605,13 @@
         return carry
 
     for part, (first, count) in enumerate(plan.parts):
-        arrive(*back[part])
+        for kind in kinds:
+            arrive(*back[kind][part])
         lax.fori_loop(first, first + count, x_inverse, 0)
-    for copies, _ in there + back:
-        for copy in copies:
-            copy.wait_send()
+    for pieces in there + back:
+        for copies, _ in pieces:
+            for copy in copies:
+                copy.wait_send()
 
 
 def gather_kernel(plan, counts_ref, atoms_ref, pot_ref, out_ref, list_ref, y_ref, x_ref, p_ref):
@@ -609,7 +648,7 @@
         totals = [weight_z * total_x, weight_z * total_y, slope_z * total_z]
         for dim in range(3):
             row = jnp.sum(totals[dim], axis=0, keepdims=True)
-            out_ref[block, pl.ds(dim * plan.chunks + chunk, 1), :] += row
+            out_ref[lax.rem(block, plan.nx), block // plan.nx, pl.ds(dim * plan.chunks + chunk, 1), :] += row
 
     over_units(plan, counts_ref, list_ref, work)
 
@@ -654,7 +693,19 @@
     counted = jnp.sum((key[None, :] < jnp.asarray(edges)[:, None]).astype(f32), axis=1)
     counted = jnp.pad(counted, (0, capacity - LANES))
     atoms = jnp.stack([t_x, t_y, t_z, charge, local_x, local_y, key.astype(f32), counted])
-    atoms = exchange(atoms, group_of("gz", "gx"), 0, same=True)
+    across, along = group_of("gz"), group_of("gx")
+    most = max(plan.nz, plan.nx)
+    atoms = vmem_call(
+        functools.partial(atoms_kernel, across, along),
+        jax.ShapeDtypeStruct((plan.blocks,) + atoms.shape, f32),
+        [
+            pltpu.SemaphoreType.DMA((plan.nz + 1, most)),
+            pltpu.SemaphoreType.DMA((plan.nz + 1, most)),
+            pltpu.SemaphoreType.DMA,
+        ],
+        collective_id=0,
+        has_side_effects=True,
+    )(atoms)
     counts = atoms[:, 7, :LANES].astype(jnp.int32)
 
     lanes = plan.tiles * LANES
@@ -684,12 +735,12 @@
             half,
             half,
             half,
-            pltpu.VMEM((plan.most * plan.nx * plan.row_k, 2 * LANES), bf16),
-            pltpu.VMEM((plan.most * plan.nx * plan.row_k, LANES), f32),
-            pltpu.VMEM((2, plan.all_y * plan.pad_k, LANES), f32),
-            pltpu.SemaphoreType.DMA((2, parts, group.count)),
-            pltpu.SemaphoreType.DMA((2, parts, group.count)),
-            pltpu.SemaphoreType.DMA((2, parts)),
+            pltpu.VMEM((plan.rows, 2 * LANES), bf16),
+            pltpu.VMEM((plan.rows, LANES), f32),
+            pltpu.VMEM((plan.groups, plan.all_y * SUBLANES, LANES), f32),
+            pltpu.SemaphoreType.DMA((2, plan.groups, parts, group.count)),
+            pltpu.SemaphoreType.DMA((2, plan.groups, parts, group.count)),
+            pltpu.SemaphoreType.DMA((2, plan.groups, parts)),
         ],
         smem=(5,),
         collective_id=1,
@@ -707,7 +758,7 @@
     )
     shares = vmem_call(
         functools.partial(gather_kernel, plan),
-        jax.ShapeDtypeStruct((plan.blocks, 3 * plan.chunks, LANES), f32),
+        jax.ShapeDtypeStruct((plan.nx, plan.nz, 3 * plan.chunks, LANES), f32),
         [
             pltpu.SMEM((units,), jnp.int32),
             pltpu.VMEM((plan.unroll, 2, plan.pad_y, LANES), f32),
@@ -716,8 +767,21 @@
         ],
         smem=(0,),
     )(counts, atoms, potential)
-    shares = exchange(shares, group_of("gz", "gx"), 2)
-    forces = -charge[None, :] * jnp.sum(shares, axis=0).reshape(3, capacity)
+    share = shares.shape[2:]
+    total = vmem_call(
+        functools.partial(shares_kernel, across, along),
+        jax.ShapeDtypeStruct(share, f32),
+        [
+            pltpu.VMEM((plan.nz,) + share, f32),
+            pltpu.VMEM(shares.shape, f32),
+            pltpu.VMEM((plan.nz,) + share, f32),
+            pltpu.SemaphoreType.DMA((2, most)),
+            pltpu.SemaphoreType.DMA((2, most)),
+        ],
+        collective_id=2,
+        has_side_effects=True,
+    )(shares)
+    forces = -charge[None, :] * total.reshape(3, capacity)
     result = lax.sort([slot, forces[0], forces[1], forces[2]], num_keys=1, is_stable=False)
     return jnp.stack(result[1:])
 

time: 155 us -> 132 us (0.85)
  Pallas kernels: 135 us -> 117 us
  local copies, waits for them, and re-layouts: 4.16 us -> 1.1 us
    pallas_call x2 -> x0, Pallas kernels: 31.5 us -> none  [exchange(): pl.pallas_call(functools.partial(exchange_kernel, group, same), in_specs=...]
    pallas_call x3 -> x5, Pallas kernels: 104 us -> 117 us  [call(): pl.pallas_call(kernel, in_specs=specs, out_specs=pl.BlockSpec(memory_spac...]
    unnamed x22 -> x16, local copies, waits for them, and re-layouts: 1.74 us -> 0.04 us
where the time goes in v3:
time: 132 us
  Pallas kernels  117 us (89%)
  other arithmetic  12.6 us (10%)
    pallas_call x5, Pallas kernels, call(): pl.pallas_call(kernel, in_specs=specs, out_specs=pl.BlockSpec(memory_spac...  117 us
    sort x1, other arithmetic, per_device(): lax.sort([slot, forces[0], forces[1], forces[2]], num_keys=1, is_stable=F...  4.89 us
    sort x1, other arithmetic, per_device(): lax.sort([key, slot, fractions[0], fractions[1], fractions[2], charge, lo...  4.33 us

profile of v3, /device:TPU:0, one launch (start us, length us, event | category | flops | bytes accessed | tf_op | source)
XLA Modules:
  0.0 131.9 jit_solution(1084352026596259885)
XLA Ops:
  0.0 0.0 copy-start.2
  0.0 0.0 copy-start.1
  0.8 0.9 fusion
  1.7 0.9 subtract_convert_fusion
  2.7 0.9 fusion.3
  3.6 4.3 %sort.78 = (s32[2048]{0:T(1024)S(1)}, s32[2048]{0:T(1024)S(1)}, f32[2048]{0:T(1024)S(1)}, f32[2048]{0:T(1024)S(1)}, f32[2048]{0:T(1024)S(1)}, /*index=5*/f32[2048]{0:T(1024)S(1)}, f32[2048]{0:T(1024)S(1)}, f32[2048]{0:T(1024)S(1)}) sort(s32[2048]{0:T(1024)S(1)} %fusion.1, s32[2048]{0:T(1024)S(1)} %iota.6, f32[2048]{0:T(1024)S(1)} %bitcast.36, ...), dimensions={0}, to_apply=%region_0.1 | sort | flops 22528 | bytes 131072 | tf_op jit(solution)/shard_map/sort | solution.py:684
  7.9 0.9 convert_reduce_fusion
  8.8 0.1 stack.59.src_ref
  8.9 0.0 copy-start.5
  8.9 13.9 %shard_map.154.atoms_ref = f32[8,8,2048]{2,1,0:T(8,128)S(1)} custom-call(f32[8,2048]{1,0:T(8,128)S(1)} %stack.59.src_ref), custom_call_target="tpu_custom_call" | custom-call | tf_op jit(solution)/shard_map/pallas_call | solution.py:662
  22.8 15.0 %shard_map.155.grid_ref = f32[4,544,512]{2,1,0:T(8,128)} custom-call(s32[8,128]{1,0:T(8,128)S(1)} %convert_bitcast_fusion.counts_ref, f32[8,8,2048]{2,1,0:T(8,128)S(1)} %shard_map.154.atoms_ref), custom_call_target="tpu_custom_call" | custom-call | tf_op jit(solution)/shard_map/pallas_call | solution.py:662
  37.8 0.0 copy-done.3
  37.8 0.0 copy-done
  37.8 0.0 copy-done.4
  37.8 0.0 copy-done.6
  37.9 0.0 copy-done.7
  37.9 0.0 copy-done.2
  37.9 0.0 copy-done.1
  37.9 0.0 copy-done.5
  37.9 65.6 %shard_map.156.pot_ref = bf16[4,544,1024]{2,1,0:T(8,128)(2,1)} custom-call(f32[4,544,512]{2,1,0:T(8,128)} %shard_map.155.grid_ref, bf16[2,256,512]{2,1,0:T(8,128)(2,1)S(1)} %copy-done.4, bf16[2,2,2,128,256]{4,3,2,1,0:T(8,128)(2,1)S(1)} %copy-done.3, bf16[2,256,544]{2,1,0:T(8,128)(2,1)S(1)} %copy-done.1, bf16[2,272,512]{2,1,0:T(8,128)(2,1)S(1)} %copy-done.2, ...), custom_call_target="tpu_custom_call" | custom-call | tf_op jit(solution)/shard_map/pallas_call | solution.py:662
  103.5 13.3 %shard_map.157.src_ref = f32[4,2,48,128]{3,2,1,0:T(8,128)S(1)} custom-call(s32[8,128]{1,0:T(8,128)S(1)} %convert_bitcast_fusion.counts_ref, f32[8,8,2048]{2,1,0:T(8,128)S(1)} %shard_map.154.atoms_ref, bf16[4,544,1024]{2,1,0:T(8,128)(2,1)} %shard_map.156.pot_ref), custom_call_target="tpu_custom_call" | custom-call | tf_op jit(solution)/shard_map/pallas_call | solution.py:662
  116.8 9.4 %shard_map.158 = f32[48,128]{1,0:T(8,128)S(1)} custom-call(f32[4,2,48,128]{3,2,1,0:T(8,128)S(1)} %shard_map.157.src_ref), custom_call_target="tpu_custom_call" | custom-call | tf_op jit(solution)/shard_map/pallas_call | solution.py:662
  126.4 4.9 %sort.79 = (s32[2048]{0:T(1024)}, f32[2048]{0:T(1024)S(1)}, f32[2048]{0:T(1024)S(1)}, f32[2048]{0:T(1024)S(1)}) sort(s32[2048]{0:T(1024)S(1)} %get-tuple-element.16, f32[2048]{0:T(1024)S(1)} %bitcast.34, f32[2048]{0:T(1024)S(1)} %bitcast.33, f32[2048]{0:T(1024)S(1)} %bitcast.32), dimensions={0}, to_apply=%region_2.3 | sort | flops 22528 | bytes 65536 | tf_op jit(solution)/shard_map/sort | solution.py:785
  131.2 0.6 pad_maximum_fusion
  (15 shorter events, 0.1 us)
Async XLA Ops:
  0.0 37.8 %copy-start.3 = (bf16[2,2,2,128,256]{4,3,2,1,0:T(8,128)(2,1)S(1)}, bf16[2,2,2,128,256]{4,3,2,1,0:T(8,128)(2,1)}, u32[]{:S(2)}) copy-start(bf16[2,2,2,128,256]{4,3,2,1,0:T(8,128)(2,1)} %constant.62.z_table_ref) | copy-start | bytes 1572868
  0.0 37.8 %copy-start = (bf16[2,256,1024]{2,1,0:T(8,128)(2,1)S(1)}, bf16[2,256,1024]{2,1,0:T(8,128)(2,1)}, u32[]{:S(2)}) copy-start(bf16[2,256,1024]{2,1,0:T(8,128)(2,1)} %constant.54.clone.x_inverse_ref) | copy-start | bytes 3145732
  0.0 37.8 %copy-start.4 = (bf16[2,256,512]{2,1,0:T(8,128)(2,1)S(1)}, bf16[2,256,512]{2,1,0:T(8,128)(2,1)}, u32[]{:S(2)}) copy-start(bf16[2,256,512]{2,1,0:T(8,128)(2,1)} %constant.50.clone.x_forward_ref) | copy-start | bytes 1572868
  0.0 37.8 %copy-start.6 = (f32[2,2,1,128]{3,2,1,0:T(1,128)S(1)}, f32[2,2,1,128]{3,2,1,0:T(1,128)}, u32[]{:S(2)}) copy-start(f32[2,2,1,128]{3,2,1,0:T(1,128)} %constant.49.clone.line_z_ref) | copy-start | bytes 6148
  0.0 37.8 %copy-start.7 = (f32[2,128]{1,0:T(2,128)S(1)}, f32[2,128]{1,0:T(2,128)}, u32[]{:S(2)}) copy-start(f32[2,128]{1,0:T(2,128)} %constant.47.clone.line_x_ref) | copy-start | bytes 3076
  0.0 37.8 %copy-start.2 = (bf16[2,272,512]{2,1,0:T(8,128)(2,1)S(1)}, bf16[2,272,512]{2,1,0:T(8,128)(2,1)}, u32[]{:S(2)}) copy-start(bf16[2,272,512]{2,1,0:T(8,128)(2,1)} %constant.46.clone.y_inverse_ref) | copy-start | bytes 1671172
  0.0 37.8 %copy-start.1 = (bf16[2,256,544]{2,1,0:T(8,128)(2,1)S(1)}, bf16[2,256,544]{2,1,0:T(8,128)(2,1)}, u32[]{:S(2)}) copy-start(bf16[2,256,544]{2,1,0:T(8,128)(2,1)} %constant.45.clone.y_forward_ref) | copy-start | bytes 1671172
  8.9 29.0 %copy-start.5 = (f32[2,256,1]{2,1,0:T(8,128)S(1)}, f32[2,256,1]{2,1,0:T(8,128)}, u32[]{:S(2)}) copy-start(f32[2,256,1]{2,1,0:T(8,128)} %constant.48.clone.line_y_ref) | copy-start | bytes 6148

commit v4 on v3

--- a/solution.py
+++ b/solution.py
@@ -67,8 +67,11 @@
         self.pad_x = round_up(self.span_x, SUBLANES)
         self.pack_x = round_up(3 * self.pad_x, LANES)
         self.unroll = 4
-        sizes = [len(part) for part in np.array_split(np.arange(self.tiles), 4)]
+        edges = np.round(self.tiles * np.array([0.0, 0.12, 0.36, 0.66, 1.0])).astype(int)
+        sizes = [int(size) for size in np.diff(edges)]
         self.parts = [(sum(sizes[:i]), size) for i, size in enumerate(sizes)]
+        sizes = sizes[::-1]
+        self.back_parts = [(sum(sizes[:i]), size) for i, size in enumerate(sizes)]
         assert nz == 2 and self.cells_z == LANES and self.span_x <= LANES
 
     def angle(self, outputs, inputs):
@@ -194,36 +197,43 @@
     pl.semaphore_wait(semaphore, sum(group.count - 1 for group in groups))
 
 
-def atoms_kernel(across, along, src_ref, out_ref, send_sems, recv_sems, local_sem):
+def atoms_kernel(across, along, pieces, src_ref, out_ref, send_sems, recv_sems, local_sem):
     mine = across.me() * along.count + along.me()
     greet([across, along])
-
-    def sends(group, source, place, row):
+    width = src_ref.shape[1] // pieces
+    lanes = [pl.ds(piece * width, width) for piece in range(pieces)]
+
+    def sends(group, source, place, row, piece):
         return group.copies(
-            lambda peer: source,
-            lambda me: out_ref.at[place],
-            lambda step: send_sems.at[row, step],
-            lambda step: recv_sems.at[row, step],
+            lambda peer: source.at[:, lanes[piece]],
+            lambda me: out_ref.at[place, :, lanes[piece]],
+            lambda step: send_sems.at[row, piece, step],
+            lambda step: recv_sems.at[row, piece, step],
         )
 
-    crossing = sends(across, src_ref, mine, 0)
-    direct = sends(along, src_ref, mine, 1)
-    for copy in crossing + direct:
-        copy.start()
+    crossing = [sends(across, src_ref, mine, 0, piece) for piece in range(pieces)]
+    direct = [sends(along, src_ref, mine, 1, piece) for piece in range(pieces)]
+    for copies in crossing + direct:
+        for copy in copies:
+            copy.start()
     own = pltpu.make_async_copy(src_ref, out_ref.at[mine], local_sem)
     own.start()
     forwarded = []
-    for row, (step, copy) in enumerate(zip(across.steps, crossing)):
-        copy.wait_recv()
-        theirs = across.index(across.partner(step)) * along.count + along.me()
-        forwarded += sends(along, out_ref.at[theirs], theirs, 2 + row)
-    for copy in forwarded:
-        copy.start()
+    for piece in range(pieces):
+        for row, (step, copy) in enumerate(zip(across.steps, crossing[piece])):
+            copy.wait_recv()
+            theirs = across.index(across.partner(step)) * along.count + along.me()
+            copies = sends(along, out_ref.at[theirs], theirs, 2 + row, piece)
+            for copy in copies:
+                copy.start()
+            forwarded.append(copies)
     own.wait()
-    for copy in crossing:
-        copy.wait_send()
-    for copy in direct + forwarded:
-        copy.wait()
+    for copies in crossing:
+        for copy in copies:
+            copy.wait_send()
+    for copies in direct + forwarded:
+        for copy in copies:
+            copy.wait()
 
 
 def shares_kernel(across, along, src_ref, out_ref, sum_ref, first_ref, second_ref, send_sems, recv_sems):
@@ -435,11 +445,10 @@
     row_k, nx = plan.row_k, plan.nx
     greet([group])
 
-    def sending(way, kind, part, out_ref, in_ref):
+    def sending(way, kind, slot, part, out_ref, in_ref):
         first, count = part
         lanes = pl.ds(first * LANES, count * LANES)
         rows = pl.ds(kind * SUBLANES, SUBLANES)
-        slot = plan.parts.index(part) if part in plan.parts else 0
         copies = group.copies(
             lambda peer: out_ref.at[peer, rows, lanes],
             lambda place: in_ref.at[place, rows, lanes],
@@ -482,10 +491,16 @@
     whole = [(0, plan.tiles)]
     kinds = range(plan.groups)
     there = [
-        [sending(0, kind, part, there_out_ref, there_in_ref) for part in (whole if kind else plan.parts)]
+        [
+            sending(0, kind, slot, part, there_out_ref, there_in_ref)
+            for slot, part in enumerate(whole if kind else plan.parts)
+        ]
         for kind in kinds
     ]
-    back = [[sending(1, kind, part, back_out_ref, back_in_ref) for part in plan.parts] for kind in kinds]
+    back = [
+        [sending(1, kind, slot, part, back_out_ref, back_in_ref) for slot, part in enumerate(plan.back_parts)]
+        for kind in kinds
+    ]
     for part, (first, count) in enumerate(plan.parts):
         lax.fori_loop(first, first + count, x_forward, 0)
         start(*there[0][part])
@@ -582,7 +597,7 @@
             arrive(*piece)
         each(plan.ny, z_forward, kind)
         each(min(plan.half_k, plan.width_k) // 2, columns, kind)
-        for part, piece in zip(plan.parts, back[kind]):
+        for part, piece in zip(plan.back_parts, back[kind]):
             each(plan.ny, z_backward, kind, part)
             start(*piece)
 
@@ -604,7 +619,7 @@
                 pot_ref[octet, pl.ds(row, 2 * SUBLANES), :] = jnp.concatenate(pieces, axis=0).astype(jnp.bfloat16)
         return carry
 
-    for part, (first, count) in enumerate(plan.parts):
+    for part, (first, count) in enumerate(plan.back_parts):
         for kind in kinds:
             arrive(*back[kind][part])
         lax.fori_loop(first, first + count, x_inverse, 0)
@@ -653,7 +668,7 @@
     over_units(plan, counts_ref, list_ref, work)
 
 
-def vmem_call(kernel, out_shape, scratch_shapes, smem=(), **params):
+def vmem_call(kernel, out_shape, scratch_shapes, limit, smem=(), **params):
     def call(*operands):
         specs = [
             pl.BlockSpec(memory_space=pltpu.SMEM if i in smem else pltpu.VMEM)
@@ -665,7 +680,7 @@
             out_specs=pl.BlockSpec(memory_space=pltpu.VMEM),
             out_shape=out_shape,
             scratch_shapes=scratch_shapes,
-            compiler_params=pltpu.CompilerParams(vmem_limit_bytes=50 * 2**20, **params),
+            compiler_params=pltpu.CompilerParams(vmem_limit_bytes=limit * 2**20, **params),
         )(*operands)
 
     return call
@@ -696,13 +711,14 @@
     across, along = group_of("gz"), group_of("gx")
     most = max(plan.nz, plan.nx)
     atoms = vmem_call(
-        functools.partial(atoms_kernel, across, along),
+        functools.partial(atoms_kernel, across, along, 2),
         jax.ShapeDtypeStruct((plan.blocks,) + atoms.shape, f32),
         [
-            pltpu.SemaphoreType.DMA((plan.nz + 1, most)),
-            pltpu.SemaphoreType.DMA((plan.nz + 1, most)),
+            pltpu.SemaphoreType.DMA((plan.nz + 1, 2, most)),
+            pltpu.SemaphoreType.DMA((plan.nz + 1, 2, most)),
             pltpu.SemaphoreType.DMA,
         ],
+        8,
         collective_id=0,
         has_side_effects=True,
     )(atoms)
@@ -720,6 +736,7 @@
             pltpu.VMEM((plan.unroll, 2 * LANES, 2 * LANES), bf16),
             pltpu.VMEM((plan.unroll, plan.rows, 2 * LANES), bf16),
         ],
+        16,
         smem=(0,),
     )(counts, atoms)
     y_forward, y_inverse = plan.y_tables()
@@ -742,6 +759,7 @@
             pltpu.SemaphoreType.DMA((2, plan.groups, parts, group.count)),
             pltpu.SemaphoreType.DMA((2, plan.groups, parts)),
         ],
+        28,
         smem=(5,),
         collective_id=1,
         has_side_effects=True,
@@ -765,6 +783,7 @@
             pltpu.VMEM((plan.unroll, plan.pack_x, 2 * LANES), bf16),
             pltpu.VMEM((plan.unroll, plan.rows, 2 * LANES), f32),
         ],
+        16,
         smem=(0,),
     )(counts, atoms, potential)
     share = shares.shape[2:]
@@ -778,6 +797,7 @@
             pltpu.SemaphoreType.DMA((2, most)),
             pltpu.SemaphoreType.DMA((2, most)),
         ],
+        8,
         collective_id=2,
         has_side_effects=True,
     )(shares)

time: 132 us -> 123 us (0.932)
  Pallas kernels: 117 us -> 108 us
    pallas_call x5, Pallas kernels: 117 us -> 108 us  [call(): pl.pallas_call(kernel, in_specs=specs, out_specs=pl.BlockSpec(memory_spac...]
where the time goes in v4:
time: 123 us; the launch traced here: 122 us
  Pallas kernels  108 us (88%)
  other arithmetic  12.6 us (10%)
    pallas_call x5, Pallas kernels, call(): pl.pallas_call(kernel, in_specs=specs, out_specs=pl.BlockSpec(memory_spac...  108 us
    sort x1, other arithmetic, per_device(): lax.sort([slot, forces[0], forces[1], forces[2]], num_keys=1, is_stable=F...  4.89 us
    sort x1, other arithmetic, per_device(): lax.sort([key, slot, fractions[0], fractions[1], fractions[2], charge, lo...  4.33 us

profile of v4, /device:TPU:0, one launch (start us, length us, event | category | flops | bytes accessed | tf_op | source)
XLA Modules:
  0.0 122.5 jit_solution(8353230467576360269)
XLA Ops:
  0.0 0.0 copy-start.2
  0.0 0.0 copy-start.1
  0.8 0.9 fusion
  1.7 0.9 subtract_convert_fusion
  2.7 0.9 fusion.3
  3.6 4.3 %sort.78 = (s32[2048]{0:T(1024)S(1)}, s32[2048]{0:T(1024)S(1)}, f32[2048]{0:T(1024)S(1)}, f32[2048]{0:T(1024)S(1)}, f32[2048]{0:T(1024)S(1)}, /*index=5*/f32[2048]{0:T(1024)S(1)}, f32[2048]{0:T(1024)S(1)}, f32[2048]{0:T(1024)S(1)}) sort(s32[2048]{0:T(1024)S(1)} %fusion.1, s32[2048]{0:T(1024)S(1)} %iota.6, f32[2048]{0:T(1024)S(1)} %bitcast.36, ...), dimensions={0}, to_apply=%region_0.1 | sort | flops 22528 | bytes 131072 | tf_op jit(solution)/shard_map/sort | solution.py:699
  7.9 0.9 convert_reduce_fusion
  8.8 0.1 stack.59.src_ref
  8.9 0.0 copy-start.5
  8.9 13.4 %shard_map.154.atoms_ref = f32[8,8,2048]{2,1,0:T(8,128)S(1)} custom-call(f32[8,2048]{1,0:T(8,128)S(1)} %stack.59.src_ref), custom_call_target="tpu_custom_call" | custom-call | tf_op jit(solution)/shard_map/pallas_call | solution.py:677
  22.3 13.0 %shard_map.155.grid_ref = f32[4,544,512]{2,1,0:T(8,128)S(1)} custom-call(s32[8,128]{1,0:T(8,128)S(1)} %convert_bitcast_fusion.counts_ref, f32[8,8,2048]{2,1,0:T(8,128)S(1)} %shard_map.154.atoms_ref), custom_call_target="tpu_custom_call" | custom-call | tf_op jit(solution)/shard_map/pallas_call | solution.py:677
  35.4 0.0 copy-done.3
  35.4 0.0 copy-done
  35.4 0.0 copy-done.4
  35.4 0.0 copy-done.6
  35.4 0.0 copy-done.7
  35.4 0.0 copy-done.2
  35.4 0.0 copy-done.1
  35.4 0.0 copy-done.5
  35.5 60.2 %shard_map.156.pot_ref = bf16[4,544,1024]{2,1,0:T(8,128)(2,1)S(1)} custom-call(f32[4,544,512]{2,1,0:T(8,128)S(1)} %shard_map.155.grid_ref, bf16[2,256,512]{2,1,0:T(8,128)(2,1)S(1)} %copy-done.4, bf16[2,2,2,128,256]{4,3,2,1,0:T(8,128)(2,1)S(1)} %copy-done.3, bf16[2,256,544]{2,1,0:T(8,128)(2,1)S(1)} %copy-done.1, bf16[2,272,512]{2,1,0:T(8,128)(2,1)S(1)} %copy-done.2, ...), custom_call_target="tpu_custom_call" | custom-call | tf_op jit(solution)/shard_map/pallas_call | solution.py:677
  95.7 11.6 %shard_map.157.src_ref = f32[4,2,48,128]{3,2,1,0:T(8,128)S(1)} custom-call(s32[8,128]{1,0:T(8,128)S(1)} %convert_bitcast_fusion.counts_ref, f32[8,8,2048]{2,1,0:T(8,128)S(1)} %shard_map.154.atoms_ref, bf16[4,544,1024]{2,1,0:T(8,128)(2,1)S(1)} %shard_map.156.pot_ref), custom_call_target="tpu_custom_call" | custom-call | tf_op jit(solution)/shard_map/pallas_call | solution.py:677
  107.3 9.6 %shard_map.158 = f32[48,128]{1,0:T(8,128)S(1)} custom-call(f32[4,2,48,128]{3,2,1,0:T(8,128)S(1)} %shard_map.157.src_ref), custom_call_target="tpu_custom_call" | custom-call | tf_op jit(solution)/shard_map/pallas_call | solution.py:677
  116.9 4.9 %sort.79 = (s32[2048]{0:T(1024)}, f32[2048]{0:T(1024)S(1)}, f32[2048]{0:T(1024)S(1)}, f32[2048]{0:T(1024)S(1)}) sort(s32[2048]{0:T(1024)S(1)} %get-tuple-element.16, f32[2048]{0:T(1024)S(1)} %bitcast.34, f32[2048]{0:T(1024)S(1)} %bitcast.33, f32[2048]{0:T(1024)S(1)} %bitcast.32), dimensions={0}, to_apply=%region_2.3 | sort | flops 22528 | bytes 65536 | tf_op jit(solution)/shard_map/sort | solution.py:805
  121.8 0.6 pad_maximum_fusion
  (15 shorter events, 0.1 us)
Async XLA Ops:
  0.0 35.4 %copy-start.3 = (bf16[2,2,2,128,256]{4,3,2,1,0:T(8,128)(2,1)S(1)}, bf16[2,2,2,128,256]{4,3,2,1,0:T(8,128)(2,1)}, u32[]{:S(2)}) copy-start(bf16[2,2,2,128,256]{4,3,2,1,0:T(8,128)(2,1)} %constant.62.z_table_ref) | copy-start | bytes 1572868
  0.0 35.4 %copy-start = (bf16[2,256,1024]{2,1,0:T(8,128)(2,1)S(1)}, bf16[2,256,1024]{2,1,0:T(8,128)(2,1)}, u32[]{:S(2)}) copy-start(bf16[2,256,1024]{2,1,0:T(8,128)(2,1)} %constant.54.clone.x_inverse_ref) | copy-start | bytes 3145732
  0.0 35.4 %copy-start.4 = (bf16[2,256,512]{2,1,0:T(8,128)(2,1)S(1)}, bf16[2,256,512]{2,1,0:T(8,128)(2,1)}, u32[]{:S(2)}) copy-start(bf16[2,256,512]{2,1,0:T(8,128)(2,1)} %constant.50.clone.x_forward_ref) | copy-start | bytes 1572868
  0.0 35.4 %copy-start.6 = (f32[2,2,1,128]{3,2,1,0:T(1,128)S(1)}, f32[2,2,1,128]{3,2,1,0:T(1,128)}, u32[]{:S(2)}) copy-start(f32[2,2,1,128]{3,2,1,0:T(1,128)} %constant.49.clone.line_z_ref) | copy-start | bytes 6148
  0.0 35.4 %copy-start.7 = (f32[2,128]{1,0:T(2,128)S(1)}, f32[2,128]{1,0:T(2,128)}, u32[]{:S(2)}) copy-start(f32[2,128]{1,0:T(2,128)} %constant.47.clone.line_x_ref) | copy-start | bytes 3076
  0.0 35.4 %copy-start.2 = (bf16[2,272,512]{2,1,0:T(8,128)(2,1)S(1)}, bf16[2,272,512]{2,1,0:T(8,128)(2,1)}, u32[]{:S(2)}) copy-start(bf16[2,272,512]{2,1,0:T(8,128)(2,1)} %constant.46.clone.y_inverse_ref) | copy-start | bytes 1671172
  0.0 35.4 %copy-start.1 = (bf16[2,256,544]{2,1,0:T(8,128)(2,1)S(1)}, bf16[2,256,544]{2,1,0:T(8,128)(2,1)}, u32[]{:S(2)}) copy-start(bf16[2,256,544]{2,1,0:T(8,128)(2,1)} %constant.45.clone.y_forward_ref) | copy-start | bytes 1671172
  8.9 26.5 %copy-start.5 = (f32[2,256,1]{2,1,0:T(8,128)S(1)}, f32[2,256,1]{2,1,0:T(8,128)}, u32[]{:S(2)}) copy-start(f32[2,256,1]{2,1,0:T(8,128)} %constant.48.clone.line_y_ref) | copy-start | bytes 6148

commit v5 on v4

--- a/solution.py
+++ b/solution.py
@@ -67,6 +67,7 @@
         self.pad_x = round_up(self.span_x, SUBLANES)
         self.pack_x = round_up(3 * self.pad_x, LANES)
         self.unroll = 4
+        self.pieces = 4
         edges = np.round(self.tiles * np.array([0.0, 0.12, 0.36, 0.66, 1.0])).astype(int)
         sizes = [int(size) for size in np.diff(edges)]
         self.parts = [(sum(sizes[:i]), size) for i, size in enumerate(sizes)]
@@ -187,13 +188,15 @@
         return result
 
 
-def greet(groups):
+def greet(groups, meanwhile=None):
     semaphore = pltpu.get_barrier_semaphore()
     for group in groups:
         for step in group.steps:
             pl.semaphore_signal(
                 semaphore, inc=1, device_id=group.partner(step), device_id_type=MESH
             )
+    if meanwhile is not None:
+        meanwhile()
     pl.semaphore_wait(semaphore, sum(group.count - 1 for group in groups))
 
 
@@ -236,8 +239,32 @@
             copy.wait()
 
 
-def shares_kernel(across, along, src_ref, out_ref, sum_ref, first_ref, second_ref, send_sems, recv_sems):
-    greet([across, along])
+def shares_kernel(
+    across,
+    along,
+    src_ref,
+    charge_ref,
+    slot_ref,
+    out_ref,
+    sum_ref,
+    first_ref,
+    second_ref,
+    total_ref,
+    pick_ref,
+    send_sems,
+    recv_sems,
+):
+    chunks = slot_ref.shape[0]
+    capacity = chunks * LANES
+    slots = jnp.concatenate([slot_ref[...], jnp.zeros((LANES - chunks, LANES), jnp.float32)], axis=0).T
+
+    def pick(chunk):
+        wanted = lax.broadcasted_iota(jnp.int32, (LANES, capacity), 1).astype(jnp.float32)
+        found = jnp.where(slots[:, chunk : chunk + 1] == wanted, 1.0, 0.0)
+        pick_ref[chunk * LANES : (chunk + 1) * LANES, :] = found.astype(jnp.bfloat16)
+
+    half = chunks // 2
+    greet([across, along], lambda: [pick(chunk) for chunk in range(half // 2)])
     first = along.copies(
         lambda peer: src_ref.at[peer],
         lambda me: first_ref.at[me],
@@ -246,6 +273,8 @@
     )
     for copy in first:
         copy.start()
+    for chunk in range(half // 2, half):
+        pick(chunk)
     total = src_ref[along.me()]
     for step, copy in zip(along.steps, first):
         copy.wait_recv()
@@ -259,11 +288,24 @@
     )
     for copy in second:
         copy.start()
+    for chunk in range(half, chunks):
+        pick(chunk)
     result = sum_ref[across.me()]
     for step, copy in zip(across.steps, second):
         copy.wait_recv()
         result = result + second_ref[across.index(across.partner(step))]
-    out_ref[...] = result
+    charge = charge_ref[...]
+    total_ref[...] = -(jnp.concatenate([charge] * 3, axis=0) * result)
+    lines = [total_ref[pl.ds(chunk, 3, stride=chunks), :] for chunk in range(chunks)]
+    rest = jnp.concatenate(lines, axis=1)
+    parts = []
+    for _ in range(3):
+        part = rest.astype(jnp.bfloat16).astype(jnp.float32)
+        rest = rest - part
+        parts.append(jnp.concatenate([part, jnp.zeros((SUBLANES - 3, capacity), jnp.float32)], axis=0))
+    parts.append(jnp.zeros((SUBLANES, capacity), jnp.float32))
+    product = mm(jnp.concatenate(parts, axis=0).astype(jnp.bfloat16), pick_ref[...])
+    out_ref[...] = product[0:3] + (product[SUBLANES : SUBLANES + 3] + product[2 * SUBLANES : 2 * SUBLANES + 3])
     for copy in first + second:
         copy.wait_send()
 
@@ -443,7 +485,6 @@
     parity = lax.axis_index("gz")
     device = group.me()
     row_k, nx = plan.row_k, plan.nx
-    greet([group])
 
     def sending(way, kind, slot, part, out_ref, in_ref):
         first, count = part
@@ -502,7 +543,10 @@
         for kind in kinds
     ]
     for part, (first, count) in enumerate(plan.parts):
-        lax.fori_loop(first, first + count, x_forward, 0)
+        if part == 0:
+            greet([group], lambda: lax.fori_loop(first, first + count, x_forward, 0))
+        else:
+            lax.fori_loop(first, first + count, x_forward, 0)
         start(*there[0][part])
     for kind in kinds[1:]:
         start(*there[kind][0])
@@ -711,11 +755,11 @@
     across, along = group_of("gz"), group_of("gx")
     most = max(plan.nz, plan.nx)
     atoms = vmem_call(
-        functools.partial(atoms_kernel, across, along, 2),
+        functools.partial(atoms_kernel, across, along, plan.pieces),
         jax.ShapeDtypeStruct((plan.blocks,) + atoms.shape, f32),
         [
-            pltpu.SemaphoreType.DMA((plan.nz + 1, 2, most)),
-            pltpu.SemaphoreType.DMA((plan.nz + 1, 2, most)),
+            pltpu.SemaphoreType.DMA((plan.nz + 1, plan.pieces, most)),
+            pltpu.SemaphoreType.DMA((plan.nz + 1, plan.pieces, most)),
             pltpu.SemaphoreType.DMA,
         ],
         8,
@@ -787,23 +831,22 @@
         smem=(0,),
     )(counts, atoms, potential)
     share = shares.shape[2:]
-    total = vmem_call(
+    return vmem_call(
         functools.partial(shares_kernel, across, along),
-        jax.ShapeDtypeStruct(share, f32),
+        jax.ShapeDtypeStruct((3, capacity), f32),
         [
             pltpu.VMEM((plan.nz,) + share, f32),
             pltpu.VMEM(shares.shape, f32),
             pltpu.VMEM((plan.nz,) + share, f32),
+            pltpu.VMEM(share, f32),
+            pltpu.VMEM((capacity, capacity), bf16),
             pltpu.SemaphoreType.DMA((2, most)),
             pltpu.SemaphoreType.DMA((2, most)),
         ],
-        8,
+        24,
         collective_id=2,
         has_side_effects=True,
-    )(shares)
-    forces = -charge[None, :] * total.reshape(3, capacity)
-    result = lax.sort([slot, forces[0], forces[1], forces[2]], num_keys=1, is_stable=False)
-    return jnp.stack(result[1:])
+    )(shares, charge.reshape(-1, LANES), slot.astype(f32).reshape(-1, LANES))
 
 
 def solution(mesh):

time: 123 us -> 119 us (0.967)
  other arithmetic: 12.6 us -> 7.04 us
    sort x1 -> x0, other arithmetic: 4.89 us -> none  [per_device(): lax.sort([slot, forces[0], forces[1], forces[2]], num_keys=1, is_stable=F...]
    pallas_call x5, Pallas kernels: 108 us -> 109 us  [call(): pl.pallas_call(kernel, in_specs=specs, out_specs=pl.BlockSpec(memory_spac...]
where the time goes in v5:
time: 119 us
  Pallas kernels  109 us (92%)
  other arithmetic  7.04 us (6%)
  local copies, waits for them, and re-layouts  1.68 us (1%)
    pallas_call x5, Pallas kernels, call(): pl.pallas_call(kernel, in_specs=specs, out_specs=pl.BlockSpec(memory_spac...  109 us
    sort x1, other arithmetic, per_device(): lax.sort([key, slot, fractions[0], fractions[1], fractions[2], charge, lo...  4.33 us

profile of v5, /device:TPU:0, one launch (start us, length us, event | category | flops | bytes accessed | tf_op | source)
XLA Modules:
  0.0 119.0 jit_solution(2257487485763158704)
XLA Ops:
  0.0 0.0 copy-start.3
  0.0 0.0 copy-start.2
  0.0 0.0 copy-start.1
  0.8 0.9 fusion
  1.7 0.9 subtract_convert_fusion
  2.7 0.9 fusion.2
  3.6 4.3 %sort.51 = (s32[2048]{0:T(1024)S(1)}, s32[2048]{0:T(1024)S(1)}, f32[2048]{0:T(1024)S(1)}, f32[2048]{0:T(1024)S(1)}, f32[2048]{0:T(1024)S(1)}, /*index=5*/f32[2048]{0:T(1024)S(1)}, f32[2048]{0:T(1024)S(1)}, f32[2048]{0:T(1024)S(1)}) sort(s32[2048]{0:T(1024)S(1)} %fusion.1, s32[2048]{0:T(1024)S(1)} %iota.6, f32[2048]{0:T(1024)S(1)} %bitcast.31, ...), dimensions={0}, to_apply=%region_0.1 | sort | flops 22528 | bytes 131072 | tf_op jit(solution)/shard_map/sort | solution.py:743
  7.9 0.9 convert_reduce_fusion
  8.8 0.1 stack.50.src_ref
  8.9 0.0 copy-start.5
  8.9 13.6 %shard_map.154.atoms_ref = f32[8,8,2048]{2,1,0:T(8,128)S(1)} custom-call(f32[8,2048]{1,0:T(8,128)S(1)} %stack.50.src_ref), custom_call_target="tpu_custom_call" | custom-call | tf_op jit(solution)/shard_map/pallas_call | solution.py:721
  22.6 12.4 %shard_map.155.grid_ref = f32[4,544,512]{2,1,0:T(8,128)S(1)} custom-call(s32[8,128]{1,0:T(8,128)S(1)} %convert_bitcast_fusion.1.counts_ref, f32[8,8,2048]{2,1,0:T(8,128)S(1)} %shard_map.154.atoms_ref), custom_call_target="tpu_custom_call" | custom-call | tf_op jit(solution)/shard_map/pallas_call | solution.py:721
  35.0 0.0 copy-done.3
  35.0 0.0 copy-done
  35.0 0.0 copy-done.4
  35.0 0.0 copy-done.6
  35.0 0.0 copy-done.7
  35.0 0.0 copy-done.2
  35.1 0.0 copy-done.1
  35.1 0.0 copy-done.5
  35.1 60.1 %shard_map.156.pot_ref = bf16[4,544,1024]{2,1,0:T(8,128)(2,1)S(1)} custom-call(f32[4,544,512]{2,1,0:T(8,128)S(1)} %shard_map.155.grid_ref, bf16[2,256,512]{2,1,0:T(8,128)(2,1)S(1)} %copy-done.4, bf16[2,2,2,128,256]{4,3,2,1,0:T(8,128)(2,1)S(1)} %copy-done.3, bf16[2,256,544]{2,1,0:T(8,128)(2,1)S(1)} %copy-done.1, bf16[2,272,512]{2,1,0:T(8,128)(2,1)S(1)} %copy-done.2, ...), custom_call_target="tpu_custom_call" | custom-call | tf_op jit(solution)/shard_map/pallas_call | solution.py:721
  95.2 11.0 %shard_map.157.src_ref = f32[4,2,48,128]{3,2,1,0:T(8,128)S(1)} custom-call(s32[8,128]{1,0:T(8,128)S(1)} %convert_bitcast_fusion.1.counts_ref, f32[8,8,2048]{2,1,0:T(8,128)S(1)} %shard_map.154.atoms_ref, bf16[4,544,1024]{2,1,0:T(8,128)(2,1)S(1)} %shard_map.156.pot_ref), custom_call_target="tpu_custom_call" | custom-call | tf_op jit(solution)/shard_map/pallas_call | solution.py:721
  106.2 12.2 %shard_map.158 = f32[3,2048]{1,0:T(4,128)S(1)} custom-call(f32[4,2,48,128]{3,2,1,0:T(8,128)S(1)} %shard_map.157.src_ref, f32[16,128]{1,0:T(8,128)S(1)} %bitcast.24, f32[16,128]{1,0:T(8,128)S(1)} %convert_bitcast_fusion.slot_ref), custom_call_target="tpu_custom_call" | custom-call | tf_op jit(solution)/shard_map/pallas_call | solution.py:721
  118.4 0.6 copy.22
  (11 shorter events, 0.0 us)
Async XLA Ops:
  0.0 35.0 %copy-start.3 = (bf16[2,2,2,128,256]{4,3,2,1,0:T(8,128)(2,1)S(1)}, bf16[2,2,2,128,256]{4,3,2,1,0:T(8,128)(2,1)}, u32[]{:S(2)}) copy-start(bf16[2,2,2,128,256]{4,3,2,1,0:T(8,128)(2,1)} %constant.62.z_table_ref) | copy-start | bytes 1572868
  0.0 35.0 %copy-start = (bf16[2,256,1024]{2,1,0:T(8,128)(2,1)S(1)}, bf16[2,256,1024]{2,1,0:T(8,128)(2,1)}, u32[]{:S(2)}) copy-start(bf16[2,256,1024]{2,1,0:T(8,128)(2,1)} %constant.54.clone.x_inverse_ref) | copy-start | bytes 3145732
  0.0 35.0 %copy-start.4 = (bf16[2,256,512]{2,1,0:T(8,128)(2,1)S(1)}, bf16[2,256,512]{2,1,0:T(8,128)(2,1)}, u32[]{:S(2)}) copy-start(bf16[2,256,512]{2,1,0:T(8,128)(2,1)} %constant.50.clone.x_forward_ref) | copy-start | bytes 1572868
  0.0 35.0 %copy-start.6 = (f32[2,2,1,128]{3,2,1,0:T(1,128)S(1)}, f32[2,2,1,128]{3,2,1,0:T(1,128)}, u32[]{:S(2)}) copy-start(f32[2,2,1,128]{3,2,1,0:T(1,128)} %constant.49.clone.line_z_ref) | copy-start | bytes 6148
  0.0 35.0 %copy-start.7 = (f32[2,128]{1,0:T(2,128)S(1)}, f32[2,128]{1,0:T(2,128)}, u32[]{:S(2)}) copy-start(f32[2,128]{1,0:T(2,128)} %constant.47.clone.line_x_ref) | copy-start | bytes 3076
  0.0 35.0 %copy-start.2 = (bf16[2,272,512]{2,1,0:T(8,128)(2,1)S(1)}, bf16[2,272,512]{2,1,0:T(8,128)(2,1)}, u32[]{:S(2)}) copy-start(bf16[2,272,512]{2,1,0:T(8,128)(2,1)} %constant.46.clone.y_inverse_ref) | copy-start | bytes 1671172
  0.0 35.0 %copy-start.1 = (bf16[2,256,544]{2,1,0:T(8,128)(2,1)S(1)}, bf16[2,256,544]{2,1,0:T(8,128)(2,1)}, u32[]{:S(2)}) copy-start(bf16[2,256,544]{2,1,0:T(8,128)(2,1)} %constant.45.clone.y_forward_ref) | copy-start | bytes 1671172
  8.9 26.1 %copy-start.5 = (f32[2,256,1]{2,1,0:T(8,128)S(1)}, f32[2,256,1]{2,1,0:T(8,128)}, u32[]{:S(2)}) copy-start(f32[2,256,1]{2,1,0:T(8,128)} %constant.48.clone.line_y_ref) | copy-start | bytes 6148
